TPU v7x, 32 devices: a whole 2x2x4 slice. The times are simulated.
32 devices in a mesh: grp: 2 (over x), dap: 4 (over y, core), sub: 4 (over z).
Axes of the slice: x: 2, y: 2, z: 4, core: 2. Of those that a mesh axis runs over, the one named last changes fastest.
Arguments:
- alignment: bfloat16 [32, 16, 256], P(('grp', 'dap', 'sub')), parts along dimension 0, may hold values from -170 to 170
- pair_bias: bfloat16 [8, 32, 16], P(None, ('grp', 'dap', 'sub')), parts along dimension 1, may hold values from -4 to 250
- row_project: bfloat16 [256, 4, 256], replicated, may hold values from -0.375 to 0.375
- row_output: bfloat16 [256, 256], replicated, may hold values from -0.375 to 0.375
- column_project: bfloat16 [256, 4, 256], replicated, may hold values from -9 to 9
- column_output: bfloat16 [256, 256], replicated, may hold values from -0.375 to 0.375
- transition_in: bfloat16 [256, 2, 1024], replicated, may hold values from -0.375 to 0.375
- transition_out: bfloat16 [1024, 256], replicated, may hold values from -0.1875 to 0.1875
- cotangent: bfloat16 [32, 16, 256], P(('grp', 'dap', 'sub')), parts along dimension 0, may hold values from -6 to 6
Outputs:
- grad_alignment: bfloat16 [32, 16, 256], P(('grp', 'dap', 'sub')), parts along dimension 0
- grad_bias: float32 [8, 32, 16], P(None, ('grp', 'dap', 'sub')), parts along dimension 1
- grad_row_project: float32 [512, 4, 256], P(('grp', 'dap', 'sub')), parts along dimension 0
- grad_row_output: float32 [512, 256], P(('grp', 'dap', 'sub')), parts along dimension 0
- grad_column_project: float32 [512, 4, 256], P(('grp', 'dap', 'sub')), parts along dimension 0
- grad_column_output: float32 [512, 256], P(('grp', 'dap', 'sub')), parts along dimension 0
- grad_transition_in: float32 [512, 2, 1024], P(('grp', 'dap', 'sub')), parts along dimension 0
- grad_transition_out: float32 [2048, 256], P(('grp', 'dap', 'sub')), parts along dimension 0
There are 2 independent parts, one for each index of `grp`. A program takes and returns all parts, laid end to end along the dimension named above; an argument that names none is the same for every part. Nothing has to cross between parts.
All inputs are finite; a program needn't handle non-finite values.
Results may differ from a plain program's by a relative error of at most 0.019.
Values may be sent and summed in bfloat16 or wider, within the bound.
No kernel may reach another device: no remote copies, remote signals or barrier semaphores. Data moves between devices by JAX's collectives and lax.ppermute only.
A program may use at most 64 MiB of HBM per device.

v0:
```python
import jax
import jax.numpy as jnp
from jax import lax
from jax.sharding import PartitionSpec as P

C = 256
H = 8
DH = 32


EPSILON = 1e-05


def product(pattern, former, latter):
    return jnp.einsum(pattern, former, latter, preferred_element_type=jnp.float32)


def normalize(values):
    values = values.astype(jnp.float32)
    centred = values - jnp.mean(values, axis=-1, keepdims=True)
    factor = lax.rsqrt(jnp.mean(centred * centred, axis=-1, keepdims=True) + EPSILON)
    return (centred * factor, factor)


def norm_back(normed, factor, upstream):
    mean_up = jnp.mean(upstream, axis=-1, keepdims=True)
    mean_cross = jnp.mean(upstream * normed, axis=-1, keepdims=True)
    return factor * (upstream - mean_up - normed * mean_cross)


def run_items(function, arrays, sequential):
    if sequential:
        return lax.map(lambda bundle: function(*bundle), arrays)
    return jax.vmap(function)(*arrays)


def head_shares(queries, key_rows, bias_head):
    scores = product("qd,kd->qk", queries, key_rows)
    if bias_head is not None:
        scores = scores + bias_head.astype(jnp.float32)
    row_top = jnp.max(scores, axis=-1, keepdims=True)
    powered = jnp.exp(scores - row_top)
    return powered / jnp.sum(powered, axis=-1, keepdims=True)


def head_forward(queries, key_rows, values, bias_head=None):
    shares = head_shares(queries, key_rows, bias_head)
    return product("qk,kd->qd", shares.astype(jnp.bfloat16), values)


def head_backward(queries, key_rows, values, grad_blend, bias_head=None):
    shares = head_shares(queries, key_rows, bias_head)
    shares_low = shares.astype(jnp.bfloat16)
    blended = product("qk,kd->qd", shares_low, values)
    grad_shares = product("qd,kd->qk", grad_blend, values)
    grad_values = product("qk,qd->kd", shares_low, grad_blend)
    centre = jnp.sum(shares * grad_shares, axis=-1, keepdims=True)
    grad_scores = shares * (grad_shares - centre)
    grad_low = grad_scores.astype(jnp.bfloat16)
    grad_queries = product("qk,kd->qd", grad_low, key_rows)
    grad_keys = product("qk,qd->kd", grad_low, queries)
    return (blended, grad_queries, grad_keys, grad_values, grad_scores)


def item_project(normed_item, weights):
    projected = product("lc,cfhd->fhld", normed_item, weights.reshape(C, 4, H, DH))
    queries = (projected[0] * DH ** (-0.5)).astype(jnp.bfloat16)
    key_rows = projected[1].astype(jnp.bfloat16)
    values = projected[2].astype(jnp.bfloat16)
    gating = jax.nn.sigmoid(projected[3])
    return (queries, key_rows, values, gating)


def forward_item(normed_item, weights, bias_table, head_loop):
    queries, key_rows, values, gating = item_project(normed_item, weights)
    if bias_table is None:
        head_args = (queries, key_rows, values)
    else:
        head_args = (queries, key_rows, values, bias_table)
    blended = run_items(head_forward, head_args, head_loop)
    return (blended * gating).astype(jnp.bfloat16)


def backward_item(normed_item, upstream_item, weights, out_weight, bias_table, head_loop):
    queries, key_rows, values, gating = item_project(normed_item, weights)
    grad_gated = product("lc,hdc->hld", upstream_item, out_weight.reshape(H, DH, C))
    grad_blend = (grad_gated * gating).astype(jnp.bfloat16)
    if bias_table is None:
        head_args = (queries, key_rows, values, grad_blend)
    else:
        head_args = (queries, key_rows, values, grad_blend, bias_table)
    blended, grad_queries, grad_keys, grad_values, grad_scores = run_items(
        head_backward, head_args, head_loop
    )
    grad_gate = grad_gated * blended * gating * (1.0 - gating)
    grad_proj = jnp.stack(
        [grad_queries * DH ** (-0.5), grad_keys, grad_values, grad_gate], axis=0
    ).astype(jnp.bfloat16)
    if bias_table is None:
        return (grad_proj, jnp.zeros((), jnp.float32))
    return (grad_proj, grad_scores)


def section_forward(normed_low, weights, bias_table, item_loop, head_loop):

    def single(normed_item):
        return forward_item(normed_item, weights, bias_table, head_loop)

    return run_items(single, (normed_low,), item_loop)


def section_backward(
    normed_low, upstream_low, weights, out_weight, bias_table, item_loop, head_loop
):

    def single(normed_item, upstream_item):
        return backward_item(normed_item, upstream_item, weights, out_weight, bias_table, head_loop)

    if bias_table is None:
        grad_proj, unused = run_items(single, (normed_low, upstream_low), item_loop)
        return (grad_proj, None)

    def accumulate(running, bundle):
        grad_proj, grad_scores = single(bundle[0], bundle[1])
        return (running + grad_scores, grad_proj)

    bias_total, grad_proj = lax.scan(
        accumulate, jnp.zeros(bias_table.shape, jnp.float32), (normed_low, upstream_low)
    )
    return (grad_proj, bias_total)


def column_block(columns, upstream, column_project, column_output, transition_in, transition_out):
    normed_cols, scale_cols = normalize(columns)
    normed_cols_low = normed_cols.astype(jnp.bfloat16)
    column_gated = section_forward(normed_cols_low, column_project, None, False, False)
    column_update = product("bhld,hdc->blc", column_gated, column_output.reshape(H, DH, C))
    after_columns = (columns.astype(jnp.float32) + column_update).astype(jnp.bfloat16)
    normed_two, scale_two = normalize(after_columns)
    normed_two_low = normed_two.astype(jnp.bfloat16)
    pre_hidden = product("blc,cfe->blfe", normed_two_low, transition_in)
    gate_part = pre_hidden[:, :, 0]
    up_part = pre_hidden[:, :, 1]
    sigmoid_gate = jax.nn.sigmoid(gate_part)
    activated = gate_part * sigmoid_gate
    hidden = (activated * up_part).astype(jnp.bfloat16)
    raw_trans_out = product("blf,blc->fc", hidden, upstream)
    grad_hidden = product("blc,fc->blf", upstream, transition_out)
    grad_gate_part = grad_hidden * up_part * sigmoid_gate * (1.0 + gate_part * (1.0 - sigmoid_gate))
    grad_up_part = grad_hidden * activated
    grad_pre = jnp.stack([grad_gate_part, grad_up_part], axis=2).astype(jnp.bfloat16)
    raw_trans_in = product("blc,blfe->cfe", normed_two_low, grad_pre)
    grad_normed_two = product("blfe,cfe->blc", grad_pre, transition_in)
    grad_after_columns = upstream.astype(jnp.float32) + norm_back(
        normed_two, scale_two, grad_normed_two
    )
    grad_columns_low = grad_after_columns.astype(jnp.bfloat16)
    grad_proj, unused = section_backward(
        normed_cols_low, grad_columns_low, column_project, column_output, None, False, False
    )
    raw_column_output = product("bhld,blc->hdc", column_gated, grad_columns_low).reshape(H * DH, C)
    raw_column_project = product("blc,bfhld->cfhd", normed_cols_low, grad_proj).reshape(
        C, 4, H * DH
    )
    grad_normed_cols = product("bfhld,cfhd->blc", grad_proj, column_project.reshape(C, 4, H, DH))
    grad_after_rows = (
        grad_after_columns + norm_back(normed_cols, scale_cols, grad_normed_cols)
    ).astype(jnp.bfloat16)
    return (grad_after_rows, raw_column_project, raw_column_output, raw_trans_in, raw_trans_out)


def row_block(
    normed_rows,
    scale_rows,
    normed_rows_low,
    row_gated,
    grad_after_rows,
    row_project,
    row_output,
    bias_table,
):
    grad_proj, bias_total = section_backward(
        normed_rows_low, grad_after_rows, row_project, row_output, bias_table, True, True
    )
    raw_row_output = product("bhld,blc->hdc", row_gated, grad_after_rows).reshape(H * DH, C)
    raw_row_project = product("blc,bfhld->cfhd", normed_rows_low, grad_proj).reshape(C, 4, H * DH)
    grad_normed_rows = product("bfhld,cfhd->blc", grad_proj, row_project.reshape(C, 4, H, DH))
    grad_alignment = (
        grad_after_rows.astype(jnp.float32) + norm_back(normed_rows, scale_rows, grad_normed_rows)
    ).astype(jnp.bfloat16)
    return (grad_alignment, raw_row_project, raw_row_output, bias_total)


def to_columns(arranged):
    moved = lax.all_to_all(arranged, ("dap", "sub"), split_axis=1, concat_axis=0, tiled=True)
    return moved


def to_rows(arranged):
    moved = lax.all_to_all(arranged, ("dap", "sub"), split_axis=0, concat_axis=1, tiled=True)
    return moved


def shards(
    alignment,
    pair_bias,
    row_project,
    row_output,
    column_project,
    column_output,
    transition_in,
    transition_out,
    cotangent,
):
    bias_full = lax.all_gather(pair_bias, ("dap", "sub"), axis=1, tiled=True)
    upstream = jnp.swapaxes(to_columns(cotangent), 0, 1)
    normed_rows, scale_rows = normalize(alignment)
    normed_rows_low = normed_rows.astype(jnp.bfloat16)
    row_gated = section_forward(normed_rows_low, row_project, bias_full, True, True)
    row_update = product("bhld,hdc->blc", row_gated, row_output.reshape(H, DH, C))
    after_rows = (alignment.astype(jnp.float32) + row_update).astype(jnp.bfloat16)
    columns = jnp.swapaxes(to_columns(after_rows), 0, 1)
    grad_columns, raw_column_project, raw_column_output, raw_trans_in, raw_trans_out = column_block(
        columns, upstream, column_project, column_output, transition_in, transition_out
    )
    sequences = alignment.shape[0] * lax.axis_size("dap") * lax.axis_size("sub")
    residues = alignment.shape[1]
    token_scale = (sequences * residues) ** (-0.5)
    term_col_project = raw_column_project * token_scale
    term_col_output = raw_column_output * token_scale
    term_trans_in = raw_trans_in * token_scale
    term_trans_out = raw_trans_out * token_scale
    grad_after_rows = to_rows(jnp.swapaxes(grad_columns, 0, 1))
    grad_alignment, raw_row_project, raw_row_output, bias_total = row_block(
        normed_rows,
        scale_rows,
        normed_rows_low,
        row_gated,
        grad_after_rows,
        row_project,
        row_output,
        bias_full,
    )
    term_row_project = raw_row_project * token_scale
    term_row_output = raw_row_output * token_scale
    bias_term = bias_total * (residues * sequences ** (-0.5))
    grad_bias = lax.psum_scatter(bias_term, ("dap", "sub"), scatter_dimension=1, tiled=True)
    (
        grad_row_project,
        grad_row_output,
        grad_col_project,
        grad_col_output,
        grad_trans_in,
        grad_trans_out,
    ) = (
        lax.psum_scatter(term_row_project, ("dap", "sub"), scatter_dimension=0, tiled=True),
        lax.psum_scatter(term_row_output, ("dap", "sub"), scatter_dimension=0, tiled=True),
        lax.psum_scatter(term_col_project, ("dap", "sub"), scatter_dimension=0, tiled=True),
        lax.psum_scatter(term_col_output, ("dap", "sub"), scatter_dimension=0, tiled=True),
        lax.psum_scatter(term_trans_in, ("dap", "sub"), scatter_dimension=0, tiled=True),
        lax.psum_scatter(term_trans_out, ("dap", "sub"), scatter_dimension=0, tiled=True),
    )
    return (
        grad_alignment,
        grad_bias,
        grad_row_project,
        grad_row_output,
        grad_col_project,
        grad_col_output,
        grad_trans_in,
        grad_trans_out,
    )


def solution(mesh):
    in_specs = (
        P(("grp", "dap", "sub"), None, None),
        P(None, ("grp", "dap", "sub"), None),
        P(),
        P(),
        P(),
        P(),
        P(),
        P(),
        P(("grp", "dap", "sub"), None, None),
    )
    out_specs = (
        P(("grp", "dap", "sub"), None, None),
        P(None, ("grp", "dap", "sub"), None),
        P(("grp", "dap", "sub"), None, None),
        P(("grp", "dap", "sub"), None),
        P(("grp", "dap", "sub"), None, None),
        P(("grp", "dap", "sub"), None),
        P(("grp", "dap", "sub"), None, None),
        P(("grp", "dap", "sub"), None),
    )
    return jax.shard_map(shards, mesh=mesh, in_specs=in_specs, out_specs=out_specs, check_vma=False)
```

profile of v0, /device:TPU:0, one launch (start us, length us, event | category | flops | bytes accessed | tf_op | source)
XLA Modules:
  0.0 455.0 jit_solution(169206894085748915)
XLA Ops:
  7.2 0.9 convert_reduce_fusion.1
  9.1 1.3 copy.70
  10.4 1.2 fusion.166
  11.7 34.2 %all_gather.3 = bf16[8,16,16]{2,0,1:T(8,128)(2,1)S(1)} all-gather(bf16[8,1,16]{2,0,1:T(8,128)(2,1)S(1)} %copy-done.25), channel_id=1, replica_groups=mesh['grp'=2,'dap'=4,'sub'=4] {'dap','sub'}, dimensions={1}, use_global_device_ids=true | all-gather | bytes 4352 | tf_op jit(solution)/shard_map/all_gather | solution.py:215
  46.0 2.9 while.47
  51.0 3.5 all-to-all-start.1
  56.1 4.6 %all-to-all-done.1 = bf16[16,2,128]{2,1,0:T(2,128)(2,1)S(1)} async-done(((bf16[16,2,128]{2,1,0:T(2,128)(2,1)}), bf16[16,2,128]{2,1,0:T(2,128)(2,1)S(1)}, u32[]{:S(2)}, u32[]{:S(2)}) %all-to-all-start.1) | async-done | bytes 8224 | tf_op jit(solution)/shard_map/all_to_all | solution.py:195
  60.7 3.5 all-to-all-start
  67.5 2.9 all-to-all-done
  70.5 1.3 fusion.91
  71.8 1.1 fusion.162
  73.7 1.0 fusion.86
  75.5 1.2 fusion.161
  78.1 3.5 all-to-all-start.2
  81.8 2.1 convolution_multiply_fusion.2
  83.9 3.9 all-to-all-done.2
  88.1 19.6 %while.48 = (s32[]{:T(128)}, f32[8,16,32]{2,1,0:T(8,128)S(1)}, f32[8,16,32]{2,1,0:T(8,128)S(1)}, bf16[8,16,32]{2,1,0:T(8,128)(2,1)S(1)}, bf16[8,16,32]{2,1,0:T(8...) while((s32[]{:T(128)}, f32[8,16,32]{2,1,0:T(8,128)S(1)}, ...), condition=%wide.region_21.22_spmd, body=%wide.region_17.21_spmd.sunk | while | flops 103378 | bytes 123465 | solution.py:33
  108.0 1.4 convolution_multiply_fusion.3
  109.5 1.9 convolution_multiply_fusion
  111.6 0.9 convolution_multiply_fusion.4
  112.7 0.9 convolution_multiply_fusion.5
  113.7 1.3 convolution_multiply_fusion.1
  115.7 58.6 %all-reduce = f32[8,16,16]{2,0,1:T(8,128)S(1)} all-reduce(f32[8,16,16]{2,0,1:T(8,128)S(1)} %broadcast_multiply_fusion), channel_id=2, replica_groups=mesh['grp'=2,'dap'=4,'sub'=4] {'dap','sub'}, use_global_device_ids=true, to_apply=%region_24.25.clone | all-reduce | flops 2048 | bytes 16384
  174.3 1.2 constant_dynamic-slice_fusion
  176.9 1.5 copy.89
  178.4 27.1 %reduce-scatter.7.cloned.1.call-done = f32[16,4,256]{2,0,1:T(8,128)} async-done(((f32[256,4,256]{2,0,1:T(8,128)}), f32[16,4,256]{2,0,1:T(8,128)}) %reduce-scatter.7.cloned.1.call-update) | async-done | bytes 65552 | tf_op jit(solution)/shard_map/reduce_scatter | solution.py:256
  205.5 1.5 copy.88
  207.0 63.0 %reduce-scatter.15.cloned.1.call-done = f32[16,2,1024]{2,0,1:T(8,128)} async-done(((f32[256,2,1024]{2,0,1:T(8,128)}), f32[16,2,1024]{2,0,1:T(8,128)}) %reduce-scatter.15.cloned.1.call-update) | async-done | bytes 131088 | tf_op jit(solution)/shard_map/reduce_scatter | solution.py:260
  270.1 1.7 copy.90
  271.7 57.0 %reduce-scatter.13.cloned.1.call-done = f32[16,256]{1,0:T(8,128)} async-done(((f32[256,256]{1,0:T(8,128)}), f32[16,256]{1,0:T(8,128)}) %reduce-scatter.13.cloned.1.call-update) | async-done | bytes 16400 | tf_op jit(solution)/shard_map/reduce_scatter | solution.py:259
  328.7 58.7 %reduce-scatter.9.cloned.1.call-done = f32[16,256]{1,0:T(8,128)} async-done(((f32[256,256]{1,0:T(8,128)}), f32[16,256]{1,0:T(8,128)}) %reduce-scatter.9.cloned.1.call-update) | async-done | bytes 16400 | tf_op jit(solution)/shard_map/reduce_scatter | solution.py:257
  387.4 60.7 %reduce-scatter.17.cloned.1.call-done = f32[64,256]{1,0:T(8,128)} async-done(((f32[1024,256]{1,0:T(8,128)}), f32[64,256]{1,0:T(8,128)}) %reduce-scatter.17.cloned.1.call-update) | async-done | bytes 65552 | tf_op jit(solution)/shard_map/reduce_scatter | solution.py:261
  (240 shorter events, 36.1 us)
Async XLA Ops:
  7.2 59.9 %copy-start = (bf16[256,2,1024]{2,1,0:T(2,128)(2,1)S(1)}, bf16[256,2,1024]{2,1,0:T(2,128)(2,1)}, u32[]{:S(2)}) copy-start(bf16[256,2,1024]{2,1,0:T(2,128)(2,1)} %param.19) | copy-start | bytes 3145732
  7.2 41.7 %copy-start.2 = (bf16[1,16,256]{2,1,0:T(8,128)(2,1)S(1)}, bf16[1,16,256]{2,1,0:T(8,128)(2,1)}, u32[]{:S(2)}) copy-start(bf16[1,16,256]{2,1,0:T(8,128)(2,1)} %param.13) | copy-start | bytes 24580
  7.2 4.5 copy-start.25
  7.2 41.7 %copy-start.4 = (bf16[256,256]{1,0:T(8,128)(2,1)S(1)}, bf16[256,256]{1,0:T(8,128)(2,1)}, u32[]{:S(2)}) copy-start(bf16[256,256]{1,0:T(8,128)(2,1)} %param.16) | copy-start | bytes 393220
  7.2 47.2 %copy-start.1 = (bf16[256,4,256]{2,1,0:T(4,128)(2,1)S(1)}, bf16[256,4,256]{2,1,0:T(4,128)(2,1)}, u32[]{:S(2)}) copy-start(bf16[256,4,256]{2,1,0:T(4,128)(2,1)} %param.17) | copy-start | bytes 1572868
  8.2 3.5 copy-start.10
  9.1 2.6 copy-start.17
  9.1 45.7 %copy-start.14 = (bf16[1,16,256]{2,1,0:T(8,128)(2,1)S(1)}, bf16[1,16,256]{2,1,0:T(8,128)(2,1)}, u32[]{:S(2)}) copy-start(bf16[1,16,256]{2,1,0:T(8,128)(2,1)} %param.21) | copy-start | bytes 24580
  11.6 54.4 %copy-start.3 = (bf16[256,256]{1,0:T(8,128)(2,1)S(1)}, bf16[256,256]{1,0:T(8,128)(2,1)}, u32[]{:S(2)}) copy-start(bf16[256,256]{1,0:T(8,128)(2,1)} %param.18) | copy-start | bytes 393220
  48.9 17.7 %copy-start.9 = (bf16[8,16,32]{2,1,0:T(8,128)(2,1)}, bf16[8,16,32]{2,1,0:T(8,128)(2,1)S(1)}, u32[]{:S(2)}) copy-start(bf16[8,16,32]{2,1,0:T(8,128)(2,1)S(1)} %get-tuple-element.495) | copy-start | bytes 24580
  51.0 9.7 %all-to-all-start.1 = ((bf16[16,2,128]{2,1,0:T(2,128)(2,1)}), bf16[16,2,128]{2,1,0:T(2,128)(2,1)S(1)}, u32[]{:S(2)}, u32[]{:S(2)}) async-start(bf16[16,2,128]{2,1,0:T(2,128)(2,1)} %reshape.628), calls=%async_computation.1 | async-start | bytes 16384 | tf_op jit(solution)/shard_map/all_to_all | solution.py:195
  60.7 9.7 %all-to-all-start = ((bf16[16,2,128]{2,1,0:T(2,128)(2,1)}), bf16[16,2,128]{2,1,0:T(2,128)(2,1)S(1)}, u32[]{:S(2)}, u32[]{:S(2)}) async-start(bf16[16,2,128]{2,1,0:T(2,128)(2,1)} %reshape.626), calls=%async_computation | async-start | bytes 16384 | tf_op jit(solution)/shard_map/all_to_all | solution.py:195
  64.3 8.6 %copy-start.12 = (f32[16]{0:T(128)}, f32[16]{0:T(128)S(1)}, u32[]{:S(2)}) copy-start(f32[16]{0:T(128)S(1)} %broadcast_multiply_fusion.8) | copy-start | bytes 196
  66.4 6.6 %copy-start.15 = (f32[16]{0:T(128)}, f32[16]{0:T(128)S(1)}, u32[]{:S(2)}) copy-start(f32[16]{0:T(128)S(1)} %broadcast_multiply_fusion.7) | copy-start | bytes 196
  70.5 4.3 copy-start.6
  70.5 4.3 copy-start.24
  71.8 4.9 %copy-start.7 = (bf16[16,1,1024]{2,0,1:T(8,128)(2,1)}, bf16[16,1,1024]{2,0,1:T(8,128)(2,1)S(1)}, u32[]{:S(2)}) copy-start(bf16[16,1,1024]{2,0,1:T(8,128)(2,1)S(1)} %get-tuple-element.263) | copy-start | bytes 98308
  71.8 4.9 %copy-start.20 = (f32[16]{0:T(128)S(1)}, f32[16]{0:T(128)}, u32[]{:S(2)}) copy-start(f32[16]{0:T(128)} %copy-done.19) | copy-start | bytes 196
  73.0 3.8 copy-start.13
  78.1 9.7 %all-to-all-start.2 = ((bf16[16,2,128]{2,1,0:T(2,128)(2,1)}), bf16[16,2,128]{2,1,0:T(2,128)(2,1)S(1)}, u32[]{:S(2)}, u32[]{:S(2)}) async-start(bf16[16,2,128]{2,1,0:T(2,128)(2,1)} %reshape.630), calls=%async_computation.2 | async-start | bytes 16384 | tf_op jit(solution)/shard_map/all_to_all | solution.py:200
  81.6 95.3 %reduce-scatter.11.cloned.1.call-start = ((), (), s32[]{:S(2)}) async-start(), calls=%async_computation.11 | async-start | bytes 1114112 | tf_op jit(solution)/shard_map/reduce_scatter | solution.py:258
  83.8 24.2 %copy-start.11 = (f32[16]{0:T(128)S(1)}, f32[16]{0:T(128)}, u32[]{:S(2)}) copy-start(f32[16]{0:T(128)} %copy-done.10) | copy-start | bytes 196
  83.9 24.2 %copy-start.18 = (f32[16]{0:T(128)S(1)}, f32[16]{0:T(128)}, u32[]{:S(2)}) copy-start(f32[16]{0:T(128)} %copy-done.17) | copy-start | bytes 196
  83.9 121.6 %reduce-scatter.7.cloned.1.call-start = ((), (), s32[]{:S(2)}) async-start(), calls=%async_computation.9 | async-start | bytes 1114112 | tf_op jit(solution)/shard_map/reduce_scatter | solution.py:256
  88.1 21.4 %copy-start.8 = (bf16[16,1,1024]{2,0,1:T(8,128)(2,1)S(1)}, bf16[16,1,1024]{2,0,1:T(8,128)(2,1)}, u32[]{:S(2)}) copy-start(bf16[16,1,1024]{2,0,1:T(8,128)(2,1)} %copy-done.7) | copy-start | bytes 98308
  88.1 21.4 %copy-start.16 = (f32[16]{0:T(128)S(1)}, f32[16]{0:T(128)}, u32[]{:S(2)}) copy-start(f32[16]{0:T(128)} %copy-done.15) | copy-start | bytes 196
  88.1 21.4 %copy-start.22 = (f32[16]{0:T(128)S(1)}, f32[16]{0:T(128)}, u32[]{:S(2)}) copy-start(f32[16]{0:T(128)} %copy-done.21) | copy-start | bytes 196
  109.4 160.6 %reduce-scatter.15.cloned.1.call-start = ((), (), s32[]{:S(2)}) async-start(), calls=%async_computation.13 | async-start | bytes 2228224 | tf_op jit(solution)/shard_map/reduce_scatter | solution.py:260
  111.4 3.7 copy-start.26
  111.4 217.3 %reduce-scatter.13.cloned.1.call-start = ((), (), s32[]{:S(2)}) async-start(), calls=%async_computation.12 | async-start | bytes 278528 | tf_op jit(solution)/shard_map/reduce_scatter | solution.py:259
  112.6 274.9 %reduce-scatter.9.cloned.1.call-start = ((), (), s32[]{:S(2)}) async-start(), calls=%async_computation.10 | async-start | bytes 278528 | tf_op jit(solution)/shard_map/reduce_scatter | solution.py:257
  113.7 334.4 %reduce-scatter.17.cloned.1.call-start = ((), (), s32[]{:S(2)}) async-start(), calls=%async_computation.14 | async-start | bytes 1114112 | tf_op jit(solution)/shard_map/reduce_scatter | solution.py:261
  (4 other events, 5.5 us)
Sparse Core Ops, SparseCore 0:
  86.0 59.2 reduce-scatter.10
  148.9 56.5 reduce-scatter.6
  209.3 60.7 reduce-scatter.14
  274.0 54.6 reduce-scatter.12
  332.6 54.7 reduce-scatter.8
  391.5 56.5 reduce-scatter.16
where the time goes:
time: 456 us; the launch traced here: 455 us
  waiting for transfers between devices  278 us (61%)
  blocking collectives  92.8 us (20%)
  matrix products  38.8 us (9%)
  between operations  14.8 us (3%)
  local copies, waits for them, and re-layouts  12.8 us (3%)
  starting transfers between devices  10.7 us (2%)
  other arithmetic  6.65 us (1%)
    reduce_scatter x1, waiting for transfers between devices, shards(): lax.psum_scatter(term_trans_in, ('dap', 'sub'), scatter_dimension=0, tile...  63 us
    reduce_scatter x1, waiting for transfers between devices, shards(): lax.psum_scatter(term_trans_out, ('dap', 'sub'), scatter_dimension=0, til...  60.7 us
    reduce_scatter x1, waiting for transfers between devices, shards(): lax.psum_scatter(term_row_output, ('dap', 'sub'), scatter_dimension=0, ti...  58.7 us
    unnamed x1, blocking collectives  58.6 us
    reduce_scatter x1, waiting for transfers between devices, shards(): lax.psum_scatter(term_col_output, ('dap', 'sub'), scatter_dimension=0, ti...  57 us
    dot_general x86, matrix products, product(): jnp.einsum(pattern, former, latter, preferred_element_type=jnp.float32)  38.6 us
    all_gather x1, blocking collectives, shards(): bias_full = lax.all_gather(pair_bias, ('dap', 'sub'), axis=1, tiled=True)  34.2 us
    reduce_scatter x1, waiting for transfers between devices, shards(): lax.psum_scatter(term_row_project, ('dap', 'sub'), scatter_dimension=0, t...  27.1 us
  transfers between devices with their start and end apart: 9, of which 8 were waited for; matrix products, arithmetic and copies ran while one was open for 9% of the time, Pallas kernels for 0%

commit v1 on v0

--- a/solution.py
+++ b/solution.py
@@ -1,6 +1,8 @@
 import jax
 import jax.numpy as jnp
 from jax import lax
+from jax.experimental import pallas as pl
+from jax.experimental.pallas import tpu as pltpu
 from jax.sharding import PartitionSpec as P
 
 C = 256
@@ -201,7 +203,7 @@
     return moved
 
 
-def shards(
+def distributed(
     alignment,
     pair_bias,
     row_project,
@@ -272,6 +274,360 @@
     )
 
 
+GATHERED_HIDDEN_BYTES = 8 * 2**20
+
+
+def dot_nn(former, latter):
+    return lax.dot_general(
+        former, latter, (((1,), (0,)), ((), ())), preferred_element_type=jnp.float32
+    )
+
+
+def dot_nt(former, latter):
+    return lax.dot_general(
+        former, latter, (((1,), (1,)), ((), ())), preferred_element_type=jnp.float32
+    )
+
+
+def dot_tn(former, latter):
+    return lax.dot_general(
+        former, latter, (((0,), (0,)), ((), ())), preferred_element_type=jnp.float32
+    )
+
+
+def iota(shape, axis):
+    return lax.broadcasted_iota(jnp.int32, shape, axis)
+
+
+def one_hot(condition):
+    return jnp.where(condition, 1.0, 0.0).astype(jnp.bfloat16)
+
+
+def segments(values, length, join):
+    width = values.shape[-1]
+    place = iota(values.shape, 1) % length
+    step = 1
+    while step < length:
+        ahead = pltpu.roll(values, width - step, 1)
+        around = pltpu.roll(values, length - step, 1)
+        values = join(values, jnp.where(place < length - step, ahead, around))
+        step *= 2
+    return values
+
+
+def by_head(rows, length):
+    tall = jnp.concatenate([rows] * H, axis=0)
+    own = iota(tall.shape, 0) // length == iota(tall.shape, 1) // DH
+    return jnp.where(own, tall, jnp.zeros_like(tall))
+
+
+def from_heads(tall, length):
+    head = iota((length, tall.shape[1]), 1) // DH
+    kept = tall[:length]
+    for at in range(1, H):
+        kept = jnp.where(head == at, tall[at * length : (at + 1) * length], kept)
+    return kept
+
+
+def part_rows(values, length):
+    return [values[at : at + length] for at in range(0, values.shape[0], length)]
+
+
+def attend(normed_low, weights, bias_rows, length):
+    projected = [dot_nn(normed_low, weights[:, at * C : (at + 1) * C]) for at in range(4)]
+    queries = (projected[0] * DH ** (-0.5)).astype(jnp.bfloat16)
+    key_rows = projected[1].astype(jnp.bfloat16)
+    values = projected[2].astype(jnp.bfloat16)
+    gating = jax.nn.sigmoid(projected[3])
+    scores = jnp.concatenate(
+        [
+            dot_nt(query, by_head(key, length))
+            for query, key in zip(part_rows(queries, length), part_rows(key_rows, length))
+        ],
+        axis=0,
+    )
+    if bias_rows is not None:
+        scores = scores + jnp.concatenate([bias_rows] * (scores.shape[0] // length), axis=0)
+    powered = jnp.exp(scores - segments(scores, length, jnp.maximum))
+    shares = powered / segments(powered, length, jnp.add)
+    shares_low = shares.astype(jnp.bfloat16)
+    blended = jnp.concatenate(
+        [
+            dot_nn(share, by_head(value, length))
+            for share, value in zip(part_rows(shares_low, length), part_rows(values, length))
+        ],
+        axis=0,
+    )
+    gated = (blended * gating).astype(jnp.bfloat16)
+    return gated, (queries, key_rows, values, gating, shares, shares_low, blended)
+
+
+def attend_back(saved, upstream_low, out_weight, length):
+    queries, key_rows, values, gating, shares, shares_low, blended = saved
+    grad_gated = dot_nt(upstream_low, out_weight)
+    grad_blend = (grad_gated * gating).astype(jnp.bfloat16)
+    grad_shares = jnp.concatenate(
+        [
+            dot_nt(grad, by_head(value, length))
+            for grad, value in zip(part_rows(grad_blend, length), part_rows(values, length))
+        ],
+        axis=0,
+    )
+    grad_scores = shares * (grad_shares - segments(shares * grad_shares, length, jnp.add))
+    grad_low = grad_scores.astype(jnp.bfloat16)
+    grad_queries = []
+    grad_keys = []
+    grad_values = []
+    for score, key, query, share, grad in zip(
+        part_rows(grad_low, length),
+        part_rows(key_rows, length),
+        part_rows(queries, length),
+        part_rows(shares_low, length),
+        part_rows(grad_blend, length),
+    ):
+        grad_queries.append(dot_nn(score, by_head(key, length)))
+        grad_keys.append(from_heads(dot_tn(score, query), length))
+        grad_values.append(from_heads(dot_tn(share, grad), length))
+    grad_gate = grad_gated * blended * gating * (1.0 - gating)
+    grad_proj = jnp.concatenate(
+        [
+            (jnp.concatenate(grad_queries, axis=0) * DH ** (-0.5)).astype(jnp.bfloat16),
+            jnp.concatenate(grad_keys, axis=0).astype(jnp.bfloat16),
+            jnp.concatenate(grad_values, axis=0).astype(jnp.bfloat16),
+            grad_gate.astype(jnp.bfloat16),
+        ],
+        axis=1,
+    )
+    return grad_proj, grad_scores
+
+
+def sample_kernel(
+    place_ref,
+    gathered_ref,
+    row_project_ref,
+    row_output_ref,
+    column_project_ref,
+    column_output_ref,
+    transition_in_ref,
+    transition_out_ref,
+    grad_alignment_ref,
+    grad_bias_ref,
+    grad_row_project_ref,
+    grad_row_output_ref,
+    grad_column_project_ref,
+    grad_column_output_ref,
+    grad_transition_in_ref,
+    grad_transition_out_ref,
+    *,
+    daps,
+    subs,
+    residues,
+):
+    sequences = gathered_ref.shape[0]
+    tokens = sequences * residues
+    hidden_units = transition_out_ref.shape[0]
+    token_scale = tokens ** (-0.5)
+    dap = place_ref[0]
+    sub = place_ref[1]
+    own = dap * subs + sub
+
+    def chosen(values, count):
+        shape = (count, values.shape[1])
+        picked = one_hot(iota(shape, 1) == iota(shape, 0) + own * count)
+        return dot_nt(picked, values).astype(jnp.bfloat16)
+
+    alignment = gathered_ref[:, :residues, :].reshape(tokens, C)
+    cotangent = gathered_ref[:, residues : 2 * residues, :].reshape(tokens, C)
+    lanes = H * residues
+    bias_blocks = gathered_ref[:, 2 * residues, :lanes]
+    from_place = iota((residues, sequences), 1)
+    from_dap = dap - from_place // subs
+    from_dap = jnp.where(from_dap < 0, from_dap + daps, from_dap)
+    from_sub = sub - from_place % subs
+    from_sub = jnp.where(from_sub < 0, from_sub + subs, from_sub)
+    bias_order = one_hot(from_dap * subs + from_sub == iota((residues, sequences), 0))
+    bias_rows = dot_nn(bias_order, bias_blocks)
+    turn = iota((tokens, tokens), 0)
+    to_columns = one_hot(
+        iota((tokens, tokens), 1) == (turn % sequences) * residues + turn // sequences
+    )
+
+    row_weights = row_project_ref[...]
+    values_in = alignment.astype(jnp.float32)
+    normed_rows, scale_rows = normalize(values_in)
+    normed_rows_low = normed_rows.astype(jnp.bfloat16)
+    row_gated, row_saved = attend(normed_rows_low, row_weights, bias_rows, residues)
+    after_rows = (values_in + dot_nn(row_gated, row_output_ref[...])).astype(jnp.bfloat16)
+
+    column_weights = column_project_ref[...]
+    columns = dot_nn(to_columns, after_rows)
+    upstream = dot_nn(to_columns, cotangent)
+    upstream_low = upstream.astype(jnp.bfloat16)
+    normed_cols, scale_cols = normalize(columns)
+    normed_cols_low = normed_cols.astype(jnp.bfloat16)
+    column_gated, column_saved = attend(normed_cols_low, column_weights, None, sequences)
+    after_columns = (columns + dot_nn(column_gated, column_output_ref[...])).astype(jnp.bfloat16)
+
+    normed_two, scale_two = normalize(after_columns)
+    normed_two_low = normed_two.astype(jnp.bfloat16)
+    chosen_two = chosen(normed_two_low, C // sequences)
+    unit_rows = hidden_units // sequences
+    chunk = min(C, hidden_units)
+    chosen_hidden = None
+    grad_normed_two = None
+    for at in range(0, hidden_units, chunk):
+        gate_weight = transition_in_ref[:, at : at + chunk]
+        up_weight = transition_in_ref[:, hidden_units + at : hidden_units + at + chunk]
+        gate_part = dot_nn(normed_two_low, gate_weight)
+        up_part = dot_nn(normed_two_low, up_weight)
+        grad_hidden = dot_nt(upstream_low, transition_out_ref[at : at + chunk, :])
+        sigmoid_gate = jax.nn.sigmoid(gate_part)
+        activated = gate_part * sigmoid_gate
+        hidden = (activated * up_part).astype(jnp.bfloat16)
+        grad_gate_part = (
+            grad_hidden * up_part * sigmoid_gate * (1.0 + gate_part * (1.0 - sigmoid_gate))
+        ).astype(jnp.bfloat16)
+        grad_up_part = (grad_hidden * activated).astype(jnp.bfloat16)
+        shape = (unit_rows, chunk)
+        picked = one_hot(iota(shape, 1) + at == iota(shape, 0) + own * unit_rows)
+        part = dot_nt(picked, hidden)
+        chosen_hidden = part if chosen_hidden is None else chosen_hidden + part
+        part = dot_nt(grad_gate_part, gate_weight) + dot_nt(grad_up_part, up_weight)
+        grad_normed_two = part if grad_normed_two is None else grad_normed_two + part
+        grad_transition_in_ref[:, 0, at : at + chunk] = (
+            dot_nn(chosen_two, grad_gate_part) * token_scale
+        )
+        grad_transition_in_ref[:, 1, at : at + chunk] = (
+            dot_nn(chosen_two, grad_up_part) * token_scale
+        )
+    grad_transition_out_ref[...] = (
+        dot_nn(chosen_hidden.astype(jnp.bfloat16), upstream_low) * token_scale
+    )
+    grad_after_columns = upstream + norm_back(normed_two, scale_two, grad_normed_two)
+
+    grad_columns_low = grad_after_columns.astype(jnp.bfloat16)
+    column_grad_proj, unused = attend_back(
+        column_saved, grad_columns_low, column_output_ref[...], sequences
+    )
+    grad_column_output_ref[...] = (
+        dot_nn(chosen(column_gated, C // sequences), grad_columns_low) * token_scale
+    )
+    raw = dot_nn(chosen(normed_cols_low, C // sequences), column_grad_proj) * token_scale
+    for at in range(4):
+        grad_column_project_ref[:, at, :] = raw[:, at * C : (at + 1) * C]
+    grad_normed_cols = dot_nt(column_grad_proj, column_weights)
+    grad_turned = (
+        grad_after_columns + norm_back(normed_cols, scale_cols, grad_normed_cols)
+    ).astype(jnp.bfloat16)
+
+    grad_after_rows = dot_tn(to_columns, grad_turned)
+    grad_rows_low = grad_after_rows.astype(jnp.bfloat16)
+    row_grad_proj, row_grad_scores = attend_back(
+        row_saved, grad_rows_low, row_output_ref[...], residues
+    )
+    grad_row_output_ref[...] = (
+        dot_nn(chosen(row_gated, C // sequences), grad_rows_low) * token_scale
+    )
+    raw = dot_nn(chosen(normed_rows_low, C // sequences), row_grad_proj) * token_scale
+    for at in range(4):
+        grad_row_project_ref[:, at, :] = raw[:, at * C : (at + 1) * C]
+    bias_total = sum(part_rows(row_grad_scores, residues)) * (residues * sequences ** (-0.5))
+    bias_own = jnp.sum(
+        jnp.where(iota(bias_total.shape, 0) == own, bias_total, 0.0), axis=0, keepdims=True
+    )
+    for at in range(H):
+        grad_bias_ref[at : at + 1, 0, :] = bias_own[:, at * residues : (at + 1) * residues]
+    grad_normed_rows = dot_nt(row_grad_proj[:residues], row_weights)
+    grad_alignment_ref[0] = (
+        grad_after_rows[:residues]
+        + norm_back(normed_rows[:residues], scale_rows[:residues], grad_normed_rows)
+    ).astype(jnp.bfloat16)
+
+
+def sample_call(daps, subs, residues, sequences, hidden_units):
+    rows = C // sequences
+    out_shape = (
+        jax.ShapeDtypeStruct((1, residues, C), jnp.bfloat16),
+        jax.ShapeDtypeStruct((H, 1, residues), jnp.float32),
+        jax.ShapeDtypeStruct((rows, 4, H * DH), jnp.float32),
+        jax.ShapeDtypeStruct((rows, C), jnp.float32),
+        jax.ShapeDtypeStruct((rows, 4, H * DH), jnp.float32),
+        jax.ShapeDtypeStruct((rows, C), jnp.float32),
+        jax.ShapeDtypeStruct((rows, 2, hidden_units), jnp.float32),
+        jax.ShapeDtypeStruct((hidden_units // sequences, C), jnp.float32),
+    )
+    return pl.pallas_call(
+        lambda *refs: sample_kernel(*refs, daps=daps, subs=subs, residues=residues),
+        out_shape=out_shape,
+        in_specs=[pl.BlockSpec(memory_space=pltpu.SMEM)]
+        + [pl.BlockSpec(memory_space=pltpu.VMEM)] * 7,
+        out_specs=tuple(pl.BlockSpec(memory_space=pltpu.VMEM) for _ in out_shape),
+        name="sample",
+    )
+
+
+def around(values, axis):
+    size = lax.axis_size(axis)
+    blocks = [values]
+    for shift in range(1, size):
+        pairs = [(source, (source + shift) % size) for source in range(size)]
+        blocks.append(lax.ppermute(values, axis, pairs))
+    return jnp.concatenate(blocks, axis=0)
+
+
+def gathered(
+    alignment,
+    pair_bias,
+    row_project,
+    row_output,
+    column_project,
+    column_output,
+    transition_in,
+    transition_out,
+    cotangent,
+):
+    daps = lax.axis_size("dap")
+    subs = lax.axis_size("sub")
+    residues = alignment.shape[1]
+    hidden_units = transition_out.shape[0]
+    bias_row = jnp.pad(pair_bias.reshape(1, 1, H * residues), ((0, 0), (0, 0), (0, C - H * residues)))
+    block = jnp.concatenate([alignment, cotangent, bias_row], axis=1)
+    blocks = around(around(block, "sub"), "dap")
+    place = jnp.stack([lax.axis_index("dap"), lax.axis_index("sub")]).astype(jnp.int32)
+    return sample_call(daps, subs, residues, daps * subs, hidden_units)(
+        place,
+        blocks,
+        row_project.reshape(C, 4 * H * DH),
+        row_output,
+        column_project.reshape(C, 4 * H * DH),
+        column_output,
+        transition_in.reshape(C, 2 * hidden_units),
+        transition_out,
+    )
+
+
+def gathered_fits(alignment, transition_out):
+    sequences = alignment.shape[0] * lax.axis_size("dap") * lax.axis_size("sub")
+    residues = alignment.shape[1]
+    hidden_bytes = sequences * residues * 2 * transition_out.shape[0] * 4
+    lengths_fit = all(
+        length >= 16 and length & (length - 1) == 0 and H * length <= C
+        for length in (sequences, residues)
+    )
+    return (
+        alignment.shape[0] == 1
+        and sequences == residues
+        and lengths_fit
+        and hidden_bytes <= GATHERED_HIDDEN_BYTES
+    )
+
+
+def shards(alignment, *others):
+    transition_out = others[-2]
+    plan = gathered if gathered_fits(alignment, transition_out) else distributed
+    return plan(alignment, *others)
+
+
 def solution(mesh):
     in_specs = (
         P(("grp", "dap", "sub"), None, None),

time: 456 us -> 36.1 us (0.08)
  waiting for transfers between devices: 278 us -> 4.82 us
  blocking collectives: 92.8 us -> 0 us
  matrix products: 38.8 us -> 0 us
  between operations: 14.8 us -> 0.71 us
  Pallas kernels: 0 us -> 13.5 us
  local copies, waits for them, and re-layouts: 12.8 us -> 5.72 us
  other arithmetic: 6.65 us -> 1.33 us
    reduce_scatter x6 -> x0, waiting for transfers between devices: 267 us -> none  [the longest x1 63 us: shards(): lax.psum_scatter(term_trans_in, ('dap', 'sub'), scatter_dimension=0, tile...]
    unnamed x1 -> x0, blocking collectives: 58.6 us -> none
    dot_general x86 -> x0, matrix products: 38.6 us -> none  [product(): jnp.einsum(pattern, former, latter, preferred_element_type=jnp.float32)]
    all_gather x1 -> x0, blocking collectives: 34.2 us -> none  [shards(): bias_full = lax.all_gather(pair_bias, ('dap', 'sub'), axis=1, tiled=True)]
    pallas_call x0 -> x1, Pallas kernels: none -> 13.5 us  [gathered(): sample_call(daps, subs, residues, daps * subs, hidden_units)]
    all_to_all x3 -> x0, waiting for transfers between devices: 11.4 us -> none  [the longest x2 7.53 us: to_columns(): lax.all_to_all(arranged, ('dap', 'sub'), split_axis=1, concat_axis=0, til...]
    all_to_all x3 -> x0, starting transfers between devices: 10.4 us -> none  [the longest x2 6.94 us: to_columns(): lax.all_to_all(arranged, ('dap', 'sub'), split_axis=1, concat_axis=0, til...]
    ppermute x0 -> x6, starting transfers between devices: none -> 9.69 us  [around(): blocks.append(lax.ppermute(values, axis, pairs))]
  transfers between devices with their start and end apart: 9 -> 6, of which waited for: 8 -> 1; matrix products, arithmetic and copies ran while one was open for 9% -> 13% of each run, Pallas kernels for 0% -> 0%
where the time goes in v1:
time: 36.1 us; the launch traced here: 35.8 us
  Pallas kernels  13.5 us (37%)
  starting transfers between devices  9.69 us (27%)
  local copies, waits for them, and re-layouts  5.72 us (16%)
  waiting for transfers between devices  4.82 us (13%)
  other arithmetic  1.33 us (4%)
  between operations  0.71 us (2%)
    pallas_call x1, Pallas kernels, gathered(): sample_call(daps, subs, residues, daps * subs, hidden_units)  13.5 us
    ppermute x6, starting transfers between devices, around(): blocks.append(lax.ppermute(values, axis, pairs))  9.69 us
    unnamed x18, local copies, waits for them, and re-layouts  4.94 us
    ppermute x6, waiting for transfers between devices, around(): blocks.append(lax.ppermute(values, axis, pairs))  4.82 us
    reshape x1, local copies, waits for them, and re-layouts, gathered(): pair_bias.reshape(1, 1, H * residues)  0.77 us
    concatenate x1, other arithmetic, gathered(): block = jnp.concatenate([alignment, cotangent, bias_row], axis=1)  0.72 us
  transfers between devices with their start and end apart: 6, of which 1 were waited for; matrix products, arithmetic and copies ran while one was open for 13% of the time, Pallas kernels for 0%

profile of v1, /device:TPU:0, one launch (start us, length us, event | category | flops | bytes accessed | tf_op | source)
XLA Modules:
  0.0 35.8 jit_solution(7202970809165584730)
XLA Ops:
  0.6 0.8 %reshape.28 = bf16[1,1,128]{2,1,0:T(2,128)(2,1)S(1)} reshape(bf16[8,1,16]{2,0,1:T(8,128)(2,1)} %param.10) | data formatting | bytes 512 | tf_op jit(solution)/shard_map/reshape | solution.py:593
  1.4 0.7 %pad_maximum_fusion.1 = (bf16[1,33,256]{2,1,0:T(8,128)(2,1)S(1)}, bf16[16,33,256]{2,1,0:T(8,128)(2,1)S(1)}) fusion(bf16[1,1,256]{2,1,0:T(2,128)(2,1)S(1)} %pad.4, bf16[1,16,256]{2,1,0:T(8,128)(2,1)} %param.17, bf16[1,16,256]{2,1,0:T(8,128)(2,1)} %param.9), kind=kLoop, calls=%fused_computation.1 | loop fusion | flops 50687 | bytes 57856 | tf_op jit(solution)/shard_map/concatenate | solution.py:594
  2.1 4.1 %collective-permute-start.1 = (bf16[1,33,256]{2,1,0:T(8,128)(2,1)S(1)}, bf16[1,33,256]{2,1,0:T(8,128)(2,1)S(1)}, u32[]{:S(2)}, u32[]{:S(2)}) collective-permute-start(bf16[1,33,256]{2,1,0:T(8,128)(2,1)S(1)} %get-tuple-element.8), channel_id=1, source_target_pairs={{0,2},{1,3},{2,0},{3,1},{4,6},{5,7},{6,4},{7,5},{8,10},{9,11},{10,... | collective-permute-start | bytes 50696 | tf_op jit(solution)/shard_map/ppermute | solution.py:574
  6.2 1.6 %collective-permute-start = (bf16[1,33,256]{2,1,0:T(8,128)(2,1)S(1)}, bf16[1,33,256]{2,1,0:T(8,128)(2,1)S(1)}, u32[]{:S(2)}, u32[]{:S(2)}) collective-permute-start(bf16[1,33,256]{2,1,0:T(8,128)(2,1)S(1)} %get-tuple-element.8), channel_id=1, source_target_pairs={{0,1},{1,2},{2,3},{3,0},{4,5},{5,6},{6,7},{7,4},{8,9},{9,10},{10,1... | collective-permute-start | bytes 50696 | tf_op jit(solution)/shard_map/ppermute | solution.py:574
  7.8 2.2 %collective-permute-start.2 = (bf16[1,33,256]{2,1,0:T(8,128)(2,1)S(1)}, bf16[1,33,256]{2,1,0:T(8,128)(2,1)S(1)}, u32[]{:S(2)}, u32[]{:S(2)}) collective-permute-start(bf16[1,33,256]{2,1,0:T(8,128)(2,1)S(1)} %get-tuple-element.8), channel_id=1, source_target_pairs={{0,3},{1,0},{2,1},{3,2},{4,7},{5,4},{6,5},{7,6},{8,11},{9,8},{10,9... | collective-permute-start | bytes 50696 | tf_op jit(solution)/shard_map/ppermute | solution.py:574
  10.0 0.0 copy-start.1
  10.0 0.6 %pad_add_fusion.refs_0_ = s32[2]{0:T(128)} fusion(s32[1]{0:T(128)} %bitcast.1, s32[1]{0:T(128)} %bitcast), kind=kLoop, calls=%fused_computation.9 | loop fusion | flops 2 | bytes 16 | tf_op jit(solution)/shard_map/stack | solution.py:596
  10.6 0.0 copy-start
  10.6 2.0 %copy.17 = bf16[32,8,4,256]{3,1,2,0:T(8,128)(2,1)} copy(bf16[32,8,4,256]{3,2,1,0:T(4,128)(2,1)} %bitcast.14) | data formatting | bytes 1048576
  12.7 0.0 copy-done.1
  12.7 0.9 %copy.18 = bf16[32,8,4,256]{3,1,2,0:T(8,128)(2,1)} copy(bf16[32,8,4,256]{3,2,1,0:T(4,128)(2,1)S(1)} %bitcast.15) | data formatting | bytes 1048576
  13.6 0.0 copy-done
  13.6 0.0 copy-start.3
  13.6 0.0 copy-start.4
  13.6 1.2 %copy.19 = bf16[32,8,2,1024]{3,1,2,0:T(8,128)(2,1)} copy(bf16[32,8,2,1024]{3,2,1,0:T(2,128)(2,1)S(1)} %bitcast.13) | data formatting | bytes 2097152
  14.8 0.0 collective-permute-done.1
  14.8 0.0 collective-permute-done
  14.8 0.0 collective-permute-done.2
  14.8 0.0 copy-done.3
  14.8 0.0 copy-done.4
  14.9 0.2 collective-permute-start.5
  15.0 1.5 %collective-permute-start.4 = (bf16[4,33,256]{2,1,0:T(8,128)(2,1)S(1)}, bf16[4,33,256]{2,1,0:T(8,128)(2,1)S(1)}, u32[]{:S(2)}, u32[]{:S(2)}) collective-permute-start(bf16[4,33,256]{2,1,0:T(8,128)(2,1)S(1)} %pad_maximum_fusion), channel_id=1, source_target_pairs={{0,8},{4,12},{8,0},{12,4},{1,9},{5,13},{9,1},{13,5},{2,10},{6,14},... | collective-permute-start | bytes 202760 | tf_op jit(solution)/shard_map/ppermute | solution.py:574
  16.5 0.2 collective-permute-start.3
  16.7 4.8 %collective-permute-done.3 = bf16[4,33,256]{2,1,0:T(8,128)(2,1)S(1)} collective-permute-done((bf16[4,33,256]{2,1,0:T(8,128)(2,1)S(1)}, bf16[4,33,256]{2,1,0:T(8,128)(2,1)S(1)}, u32[]{:S(2)}, u32[]{:S(2)}) %collective-permute-start.3) | collective-permute-done | bytes 67616 | tf_op jit(solution)/shard_map/ppermute | solution.py:574
  21.5 0.0 collective-permute-done.4
  21.5 0.0 collective-permute-done.5
  21.6 0.0 copy-start.2
  21.6 0.7 %copy-done.2 = bf16[16,33,256]{2,1,0:T(8,128)(2,1)} copy-done((bf16[16,33,256]{2,1,0:T(8,128)(2,1)}, bf16[16,33,256]{2,1,0:T(8,128)(2,1)S(1)}, u32[]{:S(2)}) %copy-start.2) | copy-done | bytes 270360
  22.3 13.5 %sample.1 = (bf16[1,16,256]{2,1,0:T(8,128)(2,1)}, f32[8,1,16]{2,1,0:T(1,128)}, f32[16,4,256]{2,1,0:T(4,128)}, f32[16,256]{1,0:T(8,128)}, f32[16,4,256]{2,1,0:T(4...) custom-call(s32[2]{0:T(128)} %pad_add_fusion.refs_0_, bf16[16,33,256]{2,1,0:T(8,128)(2,1)} %copy-done.2, ...), custom_call_target="tpu_custom_call" | custom-call | tf_op jit(solution)/shard_map/sample/pallas_call | solution.py:597
  (8 shorter events, 0.1 us)
Async XLA Ops:
  2.1 12.7 %collective-permute-start.1 = (bf16[1,33,256]{2,1,0:T(8,128)(2,1)S(1)}, bf16[1,33,256]{2,1,0:T(8,128)(2,1)S(1)}, u32[]{:S(2)}, u32[]{:S(2)}) collective-permute-start(bf16[1,33,256]{2,1,0:T(8,128)(2,1)S(1)} %get-tuple-element.8), channel_id=1, source_target_pairs={{0,2},{1,3},{2,0},{3,1},{4,6},{5,7},{6,4},{7,5},{8,10},{9,11},{10,... | collective-permute-start | bytes 50696 | tf_op jit(solution)/shard_map/ppermute | solution.py:574
  6.2 8.6 %collective-permute-start = (bf16[1,33,256]{2,1,0:T(8,128)(2,1)S(1)}, bf16[1,33,256]{2,1,0:T(8,128)(2,1)S(1)}, u32[]{:S(2)}, u32[]{:S(2)}) collective-permute-start(bf16[1,33,256]{2,1,0:T(8,128)(2,1)S(1)} %get-tuple-element.8), channel_id=1, source_target_pairs={{0,1},{1,2},{2,3},{3,0},{4,5},{5,6},{6,7},{7,4},{8,9},{9,10},{10,1... | collective-permute-start | bytes 50696 | tf_op jit(solution)/shard_map/ppermute | solution.py:574
  7.8 7.1 %collective-permute-start.2 = (bf16[1,33,256]{2,1,0:T(8,128)(2,1)S(1)}, bf16[1,33,256]{2,1,0:T(8,128)(2,1)S(1)}, u32[]{:S(2)}, u32[]{:S(2)}) collective-permute-start(bf16[1,33,256]{2,1,0:T(8,128)(2,1)S(1)} %get-tuple-element.8), channel_id=1, source_target_pairs={{0,3},{1,0},{2,1},{3,2},{4,7},{5,4},{6,5},{7,6},{8,11},{9,8},{10,9... | collective-permute-start | bytes 50696 | tf_op jit(solution)/shard_map/ppermute | solution.py:574
  10.0 2.6 %copy-start.1 = (bf16[256,4,256]{2,1,0:T(4,128)(2,1)S(1)}, bf16[256,4,256]{2,1,0:T(4,128)(2,1)}, u32[]{:S(2)}) copy-start(bf16[256,4,256]{2,1,0:T(4,128)(2,1)} %param.13) | copy-start | bytes 1572868
  10.6 2.9 %copy-start = (bf16[256,2,1024]{2,1,0:T(2,128)(2,1)S(1)}, bf16[256,2,1024]{2,1,0:T(2,128)(2,1)}, u32[]{:S(2)}) copy-start(bf16[256,2,1024]{2,1,0:T(2,128)(2,1)} %param.15) | copy-start | bytes 3145732
  13.6 1.3 %copy-start.3 = (bf16[1,16,256]{2,1,0:T(8,128)(2,1)S(1)}, bf16[1,16,256]{2,1,0:T(8,128)(2,1)}, u32[]{:S(2)}) copy-start(bf16[1,16,256]{2,1,0:T(8,128)(2,1)} %param.17) | copy-start | bytes 24580
  13.6 1.3 %copy-start.4 = (bf16[1,16,256]{2,1,0:T(8,128)(2,1)S(1)}, bf16[1,16,256]{2,1,0:T(8,128)(2,1)}, u32[]{:S(2)}) copy-start(bf16[1,16,256]{2,1,0:T(8,128)(2,1)} %param.9) | copy-start | bytes 24580
  14.9 6.7 %collective-permute-start.5 = (bf16[4,33,256]{2,1,0:T(8,128)(2,1)S(1)}, bf16[4,33,256]{2,1,0:T(8,128)(2,1)S(1)}, u32[]{:S(2)}, u32[]{:S(2)}) collective-permute-start(bf16[4,33,256]{2,1,0:T(8,128)(2,1)S(1)} %pad_maximum_fusion), channel_id=1, source_target_pairs={{0,12},{4,0},{8,4},{12,8},{1,13},{5,1},{9,5},{13,9},{2,14},{6,2},{... | collective-permute-start | bytes 202760 | tf_op jit(solution)/shard_map/ppermute | solution.py:574
  15.0 6.5 %collective-permute-start.4 = (bf16[4,33,256]{2,1,0:T(8,128)(2,1)S(1)}, bf16[4,33,256]{2,1,0:T(8,128)(2,1)S(1)}, u32[]{:S(2)}, u32[]{:S(2)}) collective-permute-start(bf16[4,33,256]{2,1,0:T(8,128)(2,1)S(1)} %pad_maximum_fusion), channel_id=1, source_target_pairs={{0,8},{4,12},{8,0},{12,4},{1,9},{5,13},{9,1},{13,5},{2,10},{6,14},... | collective-permute-start | bytes 202760 | tf_op jit(solution)/shard_map/ppermute | solution.py:574
  16.5 5.0 %collective-permute-start.3 = (bf16[4,33,256]{2,1,0:T(8,128)(2,1)S(1)}, bf16[4,33,256]{2,1,0:T(8,128)(2,1)S(1)}, u32[]{:S(2)}, u32[]{:S(2)}) collective-permute-start(bf16[4,33,256]{2,1,0:T(8,128)(2,1)S(1)} %pad_maximum_fusion), channel_id=1, source_target_pairs={{0,4},{4,8},{8,12},{12,0},{1,5},{5,9},{9,13},{13,1},{2,6},{6,10},{... | collective-permute-start | bytes 202760 | tf_op jit(solution)/shard_map/ppermute | solution.py:574
  21.6 0.7 %copy-start.2 = (bf16[16,33,256]{2,1,0:T(8,128)(2,1)}, bf16[16,33,256]{2,1,0:T(8,128)(2,1)S(1)}, u32[]{:S(2)}) copy-start(bf16[16,33,256]{2,1,0:T(8,128)(2,1)S(1)} %constant_dynamic-update-slice_fusion.refs_1_) | copy-start | bytes 811012

commit v2 on v1

--- a/solution.py
+++ b/solution.py
@@ -275,6 +275,7 @@
 
 
 GATHERED_HIDDEN_BYTES = 8 * 2**20
+KERNEL_VMEM_BYTES = 24 * 2**20
 
 
 def dot_nn(former, latter):
@@ -402,14 +403,11 @@
 
 
 def sample_kernel(
-    place_ref,
     gathered_ref,
     row_project_ref,
-    row_output_ref,
     column_project_ref,
-    column_output_ref,
     transition_in_ref,
-    transition_out_ref,
+    outputs_ref,
     grad_alignment_ref,
     grad_bias_ref,
     grad_row_project_ref,
@@ -425,10 +423,10 @@
 ):
     sequences = gathered_ref.shape[0]
     tokens = sequences * residues
-    hidden_units = transition_out_ref.shape[0]
+    hidden_units = transition_in_ref.shape[1] // 2
     token_scale = tokens ** (-0.5)
-    dap = place_ref[0]
-    sub = place_ref[1]
+    dap = lax.axis_index("dap")
+    sub = lax.axis_index("sub")
     own = dap * subs + sub
 
     def chosen(values, count):
@@ -439,25 +437,40 @@
     alignment = gathered_ref[:, :residues, :].reshape(tokens, C)
     cotangent = gathered_ref[:, residues : 2 * residues, :].reshape(tokens, C)
     lanes = H * residues
-    bias_blocks = gathered_ref[:, 2 * residues, :lanes]
-    from_place = iota((residues, sequences), 1)
-    from_dap = dap - from_place // subs
-    from_dap = jnp.where(from_dap < 0, from_dap + daps, from_dap)
+    bias_blocks = gathered_ref[:, 2 * residues :, :lanes].astype(jnp.float32)
+    bias_blocks = bias_blocks.reshape(sequences * H, lanes).astype(jnp.bfloat16)
+    spread = one_hot(iota((lanes, lanes), 0) == iota((lanes, lanes), 1) % residues)
+    bias_spread = dot_nn(bias_blocks, spread)
+    own_head = iota(bias_spread.shape, 0) % H == iota(bias_spread.shape, 1) // residues
+    bias_spread = jnp.where(own_head, bias_spread, 0.0).astype(jnp.bfloat16)
+    from_place = iota((residues, sequences * H), 1) // H
+    from_turn = from_place // subs
+    from_dap = jnp.zeros_like(from_place)
+    mask = 1
+    while mask < daps:
+        turned = from_turn // (daps // (2 * mask)) % 2
+        kept = lax.rem(dap // mask, 2)
+        from_dap = from_dap + mask * jnp.where(turned == 1, 1 - kept, kept)
+        mask *= 2
     from_sub = sub - from_place % subs
     from_sub = jnp.where(from_sub < 0, from_sub + subs, from_sub)
-    bias_order = one_hot(from_dap * subs + from_sub == iota((residues, sequences), 0))
-    bias_rows = dot_nn(bias_order, bias_blocks)
+    bias_order = one_hot(from_dap * subs + from_sub == iota(from_place.shape, 0))
+    bias_rows = dot_nn(bias_order, bias_spread)
     turn = iota((tokens, tokens), 0)
     to_columns = one_hot(
         iota((tokens, tokens), 1) == (turn % sequences) * residues + turn // sequences
     )
+
+    row_output = outputs_ref[: H * DH, :]
+    column_output = outputs_ref[H * DH : 2 * H * DH, :]
+    transition_out_at = 2 * H * DH
 
     row_weights = row_project_ref[...]
     values_in = alignment.astype(jnp.float32)
     normed_rows, scale_rows = normalize(values_in)
     normed_rows_low = normed_rows.astype(jnp.bfloat16)
     row_gated, row_saved = attend(normed_rows_low, row_weights, bias_rows, residues)
-    after_rows = (values_in + dot_nn(row_gated, row_output_ref[...])).astype(jnp.bfloat16)
+    after_rows = (values_in + dot_nn(row_gated, row_output)).astype(jnp.bfloat16)
 
     column_weights = column_project_ref[...]
     columns = dot_nn(to_columns, after_rows)
@@ -466,7 +479,7 @@
     normed_cols, scale_cols = normalize(columns)
     normed_cols_low = normed_cols.astype(jnp.bfloat16)
     column_gated, column_saved = attend(normed_cols_low, column_weights, None, sequences)
-    after_columns = (columns + dot_nn(column_gated, column_output_ref[...])).astype(jnp.bfloat16)
+    after_columns = (columns + dot_nn(column_gated, column_output)).astype(jnp.bfloat16)
 
     normed_two, scale_two = normalize(after_columns)
     normed_two_low = normed_two.astype(jnp.bfloat16)
@@ -480,7 +493,8 @@
         up_weight = transition_in_ref[:, hidden_units + at : hidden_units + at + chunk]
         gate_part = dot_nn(normed_two_low, gate_weight)
         up_part = dot_nn(normed_two_low, up_weight)
-        grad_hidden = dot_nt(upstream_low, transition_out_ref[at : at + chunk, :])
+        transition_out = outputs_ref[transition_out_at + at : transition_out_at + at + chunk, :]
+        grad_hidden = dot_nt(upstream_low, transition_out)
         sigmoid_gate = jax.nn.sigmoid(gate_part)
         activated = gate_part * sigmoid_gate
         hidden = (activated * up_part).astype(jnp.bfloat16)
@@ -507,7 +521,7 @@
 
     grad_columns_low = grad_after_columns.astype(jnp.bfloat16)
     column_grad_proj, unused = attend_back(
-        column_saved, grad_columns_low, column_output_ref[...], sequences
+        column_saved, grad_columns_low, column_output, sequences
     )
     grad_column_output_ref[...] = (
         dot_nn(chosen(column_gated, C // sequences), grad_columns_low) * token_scale
@@ -523,7 +537,7 @@
     grad_after_rows = dot_tn(to_columns, grad_turned)
     grad_rows_low = grad_after_rows.astype(jnp.bfloat16)
     row_grad_proj, row_grad_scores = attend_back(
-        row_saved, grad_rows_low, row_output_ref[...], residues
+        row_saved, grad_rows_low, row_output, residues
     )
     grad_row_output_ref[...] = (
         dot_nn(chosen(row_gated, C // sequences), grad_rows_low) * token_scale
@@ -559,9 +573,9 @@
     return pl.pallas_call(
         lambda *refs: sample_kernel(*refs, daps=daps, subs=subs, residues=residues),
         out_shape=out_shape,
-        in_specs=[pl.BlockSpec(memory_space=pltpu.SMEM)]
-        + [pl.BlockSpec(memory_space=pltpu.VMEM)] * 7,
+        in_specs=[pl.BlockSpec(memory_space=pltpu.VMEM)] * 5,
         out_specs=tuple(pl.BlockSpec(memory_space=pltpu.VMEM) for _ in out_shape),
+        compiler_params=pltpu.CompilerParams(vmem_limit_bytes=KERNEL_VMEM_BYTES),
         name="sample",
     )
 
@@ -573,6 +587,11 @@
         pairs = [(source, (source + shift) % size) for source in range(size)]
         blocks.append(lax.ppermute(values, axis, pairs))
     return jnp.concatenate(blocks, axis=0)
+
+
+def doubled(values, axis, mask):
+    pairs = [(source, source ^ mask) for source in range(lax.axis_size(axis))]
+    return jnp.concatenate([values, lax.ppermute(values, axis, pairs)], axis=0)
 
 
 def gathered(
@@ -590,20 +609,21 @@
     subs = lax.axis_size("sub")
     residues = alignment.shape[1]
     hidden_units = transition_out.shape[0]
-    bias_row = jnp.pad(pair_bias.reshape(1, 1, H * residues), ((0, 0), (0, 0), (0, C - H * residues)))
-    block = jnp.concatenate([alignment, cotangent, bias_row], axis=1)
-    blocks = around(around(block, "sub"), "dap")
-    place = jnp.stack([lax.axis_index("dap"), lax.axis_index("sub")]).astype(jnp.int32)
-    return sample_call(daps, subs, residues, daps * subs, hidden_units)(
-        place,
-        blocks,
+    bias_heads = jnp.pad(jnp.swapaxes(pair_bias, 0, 1), ((0, 0), (0, 0), (0, C - residues)))
+    block = jnp.concatenate([alignment, cotangent, bias_heads], axis=1)
+    blocks = around(lax.optimization_barrier(block), "sub")
+    weights = (
         row_project.reshape(C, 4 * H * DH),
-        row_output,
         column_project.reshape(C, 4 * H * DH),
-        column_output,
         transition_in.reshape(C, 2 * hidden_units),
-        transition_out,
-    )
+        jnp.concatenate([row_output, column_output, transition_out], axis=0),
+    )
+    blocks, weights = lax.optimization_barrier((blocks, weights))
+    mask = daps // 2
+    while mask:
+        blocks = doubled(blocks, "dap", mask)
+        mask //= 2
+    return sample_call(daps, subs, residues, daps * subs, hidden_units)(blocks, *weights)
 
 
 def gathered_fits(alignment, transition_out):
@@ -616,6 +636,7 @@
     )
     return (
         alignment.shape[0] == 1
+        and lax.axis_size("dap") & (lax.axis_size("dap") - 1) == 0
         and sequences == residues
         and lengths_fit
         and hidden_bytes <= GATHERED_HIDDEN_BYTES

time: 36.1 us -> 29.8 us (0.83)
  local copies, waits for them, and re-layouts: 5.72 us -> 1.46 us
  Pallas kernels: 13.5 us -> 11.4 us
  starting transfers between devices: 9.69 us -> 7.75 us
  waiting for transfers between devices: 4.82 us -> 6.2 us
  other arithmetic: 1.33 us -> 2.01 us
    ppermute x0 -> x2, waiting for transfers between devices: none -> 4.3 us  [doubled(): return jnp.concatenate([values, lax.ppermute(values, axis, pairs)], axis=0)]
    ppermute x6 -> x3, starting transfers between devices: 9.69 us -> 6.09 us  [around(): blocks.append(lax.ppermute(values, axis, pairs))]
    unnamed x18 -> x9, local copies, waits for them, and re-layouts: 4.94 us -> 1.46 us
    ppermute x6 -> x3, waiting for transfers between devices: 4.82 us -> 1.9 us  [around(): blocks.append(lax.ppermute(values, axis, pairs))]
    pallas_call x1, Pallas kernels: 13.5 us -> 11.4 us  [gathered(): sample_call(daps, subs, residues, daps * subs, hidden_units)]
    ppermute x0 -> x2, starting transfers between devices: none -> 1.66 us  [doubled(): return jnp.concatenate([values, lax.ppermute(values, axis, pairs)], axis=0)]
    concatenate x1 -> x4, other arithmetic: 0.72 us -> 2 us  [the longest x1 1.15 us: gathered(): jnp.concatenate([row_output, column_output, transition_out], axis=0)]
    reshape x1 -> x0, local copies, waits for them, and re-layouts: 0.77 us -> none  [gathered(): pair_bias.reshape(1, 1, H * residues)]
  transfers between devices with their start and end apart: 6 -> 5, of which waited for: 1 -> 4; matrix products, arithmetic and copies ran while one was open for 13% -> 5% of each run, Pallas kernels for 0% -> 0%
where the time goes in v2:
time: 29.8 us; the launch traced here: 29.6 us
  Pallas kernels  11.4 us (38%)
  starting transfers between devices  7.75 us (26%)
  waiting for transfers between devices  6.2 us (21%)
  other arithmetic  2.01 us (7%)
  local copies, waits for them, and re-layouts  1.46 us (5%)
  between operations  0.72 us (2%)
    pallas_call x1, Pallas kernels, gathered(): sample_call(daps, subs, residues, daps * subs, hidden_units)  11.4 us
    ppermute x3, starting transfers between devices, around(): blocks.append(lax.ppermute(values, axis, pairs))  6.09 us
    ppermute x2, waiting for transfers between devices, doubled(): return jnp.concatenate([values, lax.ppermute(values, axis, pairs)], axis=0)  4.3 us
    ppermute x3, waiting for transfers between devices, around(): blocks.append(lax.ppermute(values, axis, pairs))  1.9 us
    ppermute x2, starting transfers between devices, doubled(): return jnp.concatenate([values, lax.ppermute(values, axis, pairs)], axis=0)  1.66 us
    unnamed x9, local copies, waits for them, and re-layouts  1.46 us
    concatenate x1, other arithmetic, gathered(): jnp.concatenate([row_output, column_output, transition_out], axis=0)  1.15 us
    concatenate x1, other arithmetic, gathered(): block = jnp.concatenate([alignment, cotangent, bias_heads], axis=1)  0.79 us
  transfers between devices with their start and end apart: 5, of which 4 were waited for; matrix products, arithmetic and copies ran while one was open for 5% of the time, Pallas kernels for 0%

profile of v2, /device:TPU:0, one launch (start us, length us, event | category | flops | bytes accessed | tf_op | source)
XLA Modules:
  0.0 29.6 jit_solution(16132938098970576473)
XLA Ops:
  0.6 0.0 copy-start.1
  0.6 0.8 %fusion.1 = bf16[1,40,256]{2,1,0:T(8,128)(2,1)S(1)} fusion(bf16[1,8,16]{2,1,0:T(8,128)(2,1)} %bitcast.13, bf16[1,16,256]{2,1,0:T(8,128)(2,1)} %param.17, bf16[1,16,256]{2,1,0:T(8,128)(2,1)} %param.9), kind=kLoop, calls=%fused_computation.6 | loop fusion | flops 81920 | bytes 37120 | tf_op jit(solution)/shard_map/concatenate | solution.py:613
  1.4 0.0 copy-start.2
  1.4 5.1 %collective-permute-start.2 = (bf16[1,40,256]{2,1,0:T(8,128)(2,1)S(1)}, bf16[1,40,256]{2,1,0:T(8,128)(2,1)S(1)}, u32[]{:S(2)}, u32[]{:S(2)}) collective-permute-start(bf16[1,40,256]{2,1,0:T(8,128)(2,1)S(1)} %fusion.1), channel_id=1, source_target_pairs={{0,3},{1,0},{2,1},{3,2},{4,7},{5,4},{6,5},{7,6},{8,11},{9,8},{10,9... | collective-permute-start | bytes 61448 | tf_op jit(solution)/shard_map/ppermute | solution.py:588
  6.5 0.0 collective-permute-start.1
  6.5 1.0 %collective-permute-start = (bf16[1,40,256]{2,1,0:T(8,128)(2,1)S(1)}, bf16[1,40,256]{2,1,0:T(8,128)(2,1)S(1)}, u32[]{:S(2)}, u32[]{:S(2)}) collective-permute-start(bf16[1,40,256]{2,1,0:T(8,128)(2,1)S(1)} %fusion.1), channel_id=1, source_target_pairs={{0,1},{1,2},{2,3},{3,0},{4,5},{5,6},{6,7},{7,4},{8,9},{9,10},{10,1... | collective-permute-start | bytes 61448 | tf_op jit(solution)/shard_map/ppermute | solution.py:588
  7.5 1.2 %pad_maximum_fusion.refs_4_ = bf16[1536,256]{1,0:T(8,128)(2,1)S(1)} fusion(bf16[1024,256]{1,0:T(8,128)(2,1)} %param.16, bf16[256,256]{1,0:T(8,128)(2,1)} %param.14, bf16[256,256]{1,0:T(8,128)(2,1)} %param.12), kind=kLoop, calls=%fused_computation | loop fusion | flops 2359296 | bytes 1572864 | tf_op jit(solution)/shard_map/concatenate | solution.py:619
  8.7 0.0 copy-done.1
  8.7 0.0 copy-start
  8.7 0.1 copy.17
  8.8 0.0 copy-done.2
  8.8 0.1 copy.18
  8.9 1.0 %copy-done = bf16[256,2,1024]{2,1,0:T(2,128)(2,1)S(1)} copy-done((bf16[256,2,1024]{2,1,0:T(2,128)(2,1)S(1)}, bf16[256,2,1024]{2,1,0:T(2,128)(2,1)}, u32[]{:S(2)}) %copy-start) | copy-done | bytes 1048600
  9.9 0.3 copy.19
  10.2 0.0 collective-permute-done.2
  10.2 1.0 %collective-permute-done.1 = bf16[1,40,256]{2,1,0:T(8,128)(2,1)S(1)} collective-permute-done((bf16[1,40,256]{2,1,0:T(8,128)(2,1)S(1)}, bf16[1,40,256]{2,1,0:T(8,128)(2,1)S(1)}, u32[]{:S(2)}, u32[]{:S(2)}) %collective-permute-start.1) | collective-permute-done | bytes 20512 | tf_op jit(solution)/shard_map/ppermute | solution.py:588
  11.2 0.9 %collective-permute-done = bf16[1,40,256]{2,1,0:T(8,128)(2,1)S(1)} collective-permute-done((bf16[1,40,256]{2,1,0:T(8,128)(2,1)S(1)}, bf16[1,40,256]{2,1,0:T(8,128)(2,1)S(1)}, u32[]{:S(2)}, u32[]{:S(2)}) %collective-permute-start) | collective-permute-done | bytes 20512 | tf_op jit(solution)/shard_map/ppermute | solution.py:588
  12.1 1.6 %collective-permute-start.3 = (bf16[4,40,256]{2,1,0:T(8,128)(2,1)S(1)}, bf16[4,40,256]{2,1,0:T(8,128)(2,1)S(1)}, u32[]{:S(2)}, u32[]{:S(2)}) collective-permute-start(bf16[4,40,256]{2,1,0:T(8,128)(2,1)S(1)} %pad_maximum_fusion.3), channel_id=1, source_target_pairs={{0,8},{4,12},{8,0},{12,4},{1,9},{5,13},{9,1},{13,5},{2,10},{6,14},... | collective-permute-start | bytes 245768 | tf_op jit(solution)/shard_map/ppermute | solution.py:594
  13.7 2.9 %collective-permute-done.3 = bf16[4,40,256]{2,1,0:T(8,128)(2,1)S(1)} collective-permute-done((bf16[4,40,256]{2,1,0:T(8,128)(2,1)S(1)}, bf16[4,40,256]{2,1,0:T(8,128)(2,1)S(1)}, u32[]{:S(2)}, u32[]{:S(2)}) %collective-permute-start.3) | collective-permute-done | bytes 81952 | tf_op jit(solution)/shard_map/ppermute | solution.py:594
  16.6 0.1 collective-permute-start.4
  16.7 1.4 %collective-permute-done.4 = bf16[8,40,256]{2,1,0:T(8,128)(2,1)S(1)} collective-permute-done((bf16[8,40,256]{2,1,0:T(8,128)(2,1)S(1)}, bf16[8,40,256]{2,1,0:T(8,128)(2,1)S(1)}, u32[]{:S(2)}, u32[]{:S(2)}) %collective-permute-start.4) | collective-permute-done | bytes 163872 | tf_op jit(solution)/shard_map/ppermute | solution.py:594
  18.1 11.4 %sample.1 = (bf16[1,16,256]{2,1,0:T(8,128)(2,1)}, f32[8,1,16]{2,1,0:T(1,128)}, f32[16,4,256]{2,1,0:T(4,128)}, f32[16,256]{1,0:T(8,128)}, f32[16,4,256]{2,1,0:T(4...) custom-call(bf16[16,40,256]{2,1,0:T(8,128)(2,1)S(1)} %pad_maximum_fusion.1.refs_0_, ...), custom_call_target="tpu_custom_call" | custom-call | tf_op jit(solution)/shard_map/sample/pallas_call | solution.py:626
  (3 shorter events, 0.1 us)
Async XLA Ops:
  0.6 8.1 %copy-start.1 = (bf16[256,4,256]{2,1,0:T(4,128)(2,1)S(1)}, bf16[256,4,256]{2,1,0:T(4,128)(2,1)}, u32[]{:S(2)}) copy-start(bf16[256,4,256]{2,1,0:T(4,128)(2,1)} %param.11) | copy-start | bytes 1572868
  1.4 7.4 %copy-start.2 = (bf16[256,4,256]{2,1,0:T(4,128)(2,1)S(1)}, bf16[256,4,256]{2,1,0:T(4,128)(2,1)}, u32[]{:S(2)}) copy-start(bf16[256,4,256]{2,1,0:T(4,128)(2,1)} %param.13) | copy-start | bytes 1572868
  1.4 8.8 %collective-permute-start.2 = (bf16[1,40,256]{2,1,0:T(8,128)(2,1)S(1)}, bf16[1,40,256]{2,1,0:T(8,128)(2,1)S(1)}, u32[]{:S(2)}, u32[]{:S(2)}) collective-permute-start(bf16[1,40,256]{2,1,0:T(8,128)(2,1)S(1)} %fusion.1), channel_id=1, source_target_pairs={{0,3},{1,0},{2,1},{3,2},{4,7},{5,4},{6,5},{7,6},{8,11},{9,8},{10,9... | collective-permute-start | bytes 61448 | tf_op jit(solution)/shard_map/ppermute | solution.py:588
  6.5 4.7 %collective-permute-start.1 = (bf16[1,40,256]{2,1,0:T(8,128)(2,1)S(1)}, bf16[1,40,256]{2,1,0:T(8,128)(2,1)S(1)}, u32[]{:S(2)}, u32[]{:S(2)}) collective-permute-start(bf16[1,40,256]{2,1,0:T(8,128)(2,1)S(1)} %fusion.1), channel_id=1, source_target_pairs={{0,2},{1,3},{2,0},{3,1},{4,6},{5,7},{6,4},{7,5},{8,10},{9,11},{10,... | collective-permute-start | bytes 61448 | tf_op jit(solution)/shard_map/ppermute | solution.py:588
  6.5 5.6 %collective-permute-start = (bf16[1,40,256]{2,1,0:T(8,128)(2,1)S(1)}, bf16[1,40,256]{2,1,0:T(8,128)(2,1)S(1)}, u32[]{:S(2)}, u32[]{:S(2)}) collective-permute-start(bf16[1,40,256]{2,1,0:T(8,128)(2,1)S(1)} %fusion.1), channel_id=1, source_target_pairs={{0,1},{1,2},{2,3},{3,0},{4,5},{5,6},{6,7},{7,4},{8,9},{9,10},{10,1... | collective-permute-start | bytes 61448 | tf_op jit(solution)/shard_map/ppermute | solution.py:588
  8.7 1.2 %copy-start = (bf16[256,2,1024]{2,1,0:T(2,128)(2,1)S(1)}, bf16[256,2,1024]{2,1,0:T(2,128)(2,1)}, u32[]{:S(2)}) copy-start(bf16[256,2,1024]{2,1,0:T(2,128)(2,1)} %param.15) | copy-start | bytes 3145732
  12.1 4.5 %collective-permute-start.3 = (bf16[4,40,256]{2,1,0:T(8,128)(2,1)S(1)}, bf16[4,40,256]{2,1,0:T(8,128)(2,1)S(1)}, u32[]{:S(2)}, u32[]{:S(2)}) collective-permute-start(bf16[4,40,256]{2,1,0:T(8,128)(2,1)S(1)} %pad_maximum_fusion.3), channel_id=1, source_target_pairs={{0,8},{4,12},{8,0},{12,4},{1,9},{5,13},{9,1},{13,5},{2,10},{6,14},... | collective-permute-start | bytes 245768 | tf_op jit(solution)/shard_map/ppermute | solution.py:594
  16.6 1.5 %collective-permute-start.4 = (bf16[8,40,256]{2,1,0:T(8,128)(2,1)S(1)}, bf16[8,40,256]{2,1,0:T(8,128)(2,1)S(1)}, u32[]{:S(2)}, u32[]{:S(2)}) collective-permute-start(bf16[8,40,256]{2,1,0:T(8,128)(2,1)S(1)} %pad_maximum_fusion.2), channel_id=1, source_target_pairs={{0,4},{4,0},{8,12},{12,8},{1,5},{5,1},{9,13},{13,9},{2,6},{6,2},{1... | collective-permute-start | bytes 491528 | tf_op jit(solution)/shard_map/ppermute | solution.py:594

commit v3 on v2

--- a/solution.py
+++ b/solution.py
@@ -304,16 +304,8 @@
     return jnp.where(condition, 1.0, 0.0).astype(jnp.bfloat16)
 
 
-def segments(values, length, join):
-    width = values.shape[-1]
-    place = iota(values.shape, 1) % length
-    step = 1
-    while step < length:
-        ahead = pltpu.roll(values, width - step, 1)
-        around = pltpu.roll(values, length - step, 1)
-        values = join(values, jnp.where(place < length - step, ahead, around))
-        step *= 2
-    return values
+def grouped(values, length):
+    return values.reshape(values.shape[0] // length, length, values.shape[1])
 
 
 def by_head(rows, length):
@@ -334,7 +326,7 @@
     return [values[at : at + length] for at in range(0, values.shape[0], length)]
 
 
-def attend(normed_low, weights, bias_rows, length):
+def attend(normed_low, weights, bias_keys, length):
     projected = [dot_nn(normed_low, weights[:, at * C : (at + 1) * C]) for at in range(4)]
     queries = (projected[0] * DH ** (-0.5)).astype(jnp.bfloat16)
     key_rows = projected[1].astype(jnp.bfloat16)
@@ -342,19 +334,21 @@
     gating = jax.nn.sigmoid(projected[3])
     scores = jnp.concatenate(
         [
-            dot_nt(query, by_head(key, length))
+            dot_nt(key, by_head(query, length))
             for query, key in zip(part_rows(queries, length), part_rows(key_rows, length))
         ],
         axis=0,
     )
-    if bias_rows is not None:
-        scores = scores + jnp.concatenate([bias_rows] * (scores.shape[0] // length), axis=0)
-    powered = jnp.exp(scores - segments(scores, length, jnp.maximum))
-    shares = powered / segments(powered, length, jnp.add)
+    scores = grouped(scores, length)
+    if bias_keys is not None:
+        scores = scores + bias_keys[None]
+    powered = jnp.exp(scores - jnp.max(scores, axis=1, keepdims=True))
+    shares = powered / jnp.sum(powered, axis=1, keepdims=True)
+    shares = shares.reshape(normed_low.shape[0], H * length)
     shares_low = shares.astype(jnp.bfloat16)
     blended = jnp.concatenate(
         [
-            dot_nn(share, by_head(value, length))
+            from_heads(dot_tn(share, value), length)
             for share, value in zip(part_rows(shares_low, length), part_rows(values, length))
         ],
         axis=0,
@@ -367,28 +361,26 @@
     queries, key_rows, values, gating, shares, shares_low, blended = saved
     grad_gated = dot_nt(upstream_low, out_weight)
     grad_blend = (grad_gated * gating).astype(jnp.bfloat16)
-    grad_shares = jnp.concatenate(
-        [
-            dot_nt(grad, by_head(value, length))
-            for grad, value in zip(part_rows(grad_blend, length), part_rows(values, length))
-        ],
-        axis=0,
-    )
-    grad_scores = shares * (grad_shares - segments(shares * grad_shares, length, jnp.add))
+    grad_shares = []
+    grad_values = []
+    for share, grad, value in zip(
+        part_rows(shares_low, length), part_rows(grad_blend, length), part_rows(values, length)
+    ):
+        grad_spread = by_head(grad, length)
+        grad_shares.append(dot_nt(value, grad_spread))
+        grad_values.append(dot_nn(share, grad_spread))
+    shares = grouped(shares, length)
+    grad_shares = grouped(jnp.concatenate(grad_shares, axis=0), length)
+    centre = jnp.sum(shares * grad_shares, axis=1, keepdims=True)
+    grad_scores = (shares * (grad_shares - centre)).reshape(upstream_low.shape[0], H * length)
     grad_low = grad_scores.astype(jnp.bfloat16)
     grad_queries = []
     grad_keys = []
-    grad_values = []
-    for score, key, query, share, grad in zip(
-        part_rows(grad_low, length),
-        part_rows(key_rows, length),
-        part_rows(queries, length),
-        part_rows(shares_low, length),
-        part_rows(grad_blend, length),
+    for score, key, query in zip(
+        part_rows(grad_low, length), part_rows(key_rows, length), part_rows(queries, length)
     ):
-        grad_queries.append(dot_nn(score, by_head(key, length)))
-        grad_keys.append(from_heads(dot_tn(score, query), length))
-        grad_values.append(from_heads(dot_tn(share, grad), length))
+        grad_queries.append(from_heads(dot_tn(score, key), length))
+        grad_keys.append(dot_nn(score, by_head(query, length)))
     grad_gate = grad_gated * blended * gating * (1.0 - gating)
     grad_proj = jnp.concatenate(
         [
@@ -439,11 +431,8 @@
     lanes = H * residues
     bias_blocks = gathered_ref[:, 2 * residues :, :lanes].astype(jnp.float32)
     bias_blocks = bias_blocks.reshape(sequences * H, lanes).astype(jnp.bfloat16)
-    spread = one_hot(iota((lanes, lanes), 0) == iota((lanes, lanes), 1) % residues)
-    bias_spread = dot_nn(bias_blocks, spread)
-    own_head = iota(bias_spread.shape, 0) % H == iota(bias_spread.shape, 1) // residues
-    bias_spread = jnp.where(own_head, bias_spread, 0.0).astype(jnp.bfloat16)
-    from_place = iota((residues, sequences * H), 1) // H
+    block_at = iota((sequences * H, lanes), 0)
+    from_place = block_at // H
     from_turn = from_place // subs
     from_dap = jnp.zeros_like(from_place)
     mask = 1
@@ -454,8 +443,12 @@
         mask *= 2
     from_sub = sub - from_place % subs
     from_sub = jnp.where(from_sub < 0, from_sub + subs, from_sub)
-    bias_order = one_hot(from_dap * subs + from_sub == iota(from_place.shape, 0))
-    bias_rows = dot_nn(bias_order, bias_spread)
+    query_lane = iota(block_at.shape, 1)
+    bias_order = one_hot(
+        (from_dap * subs + from_sub == query_lane % residues)
+        & (block_at % H == query_lane // residues)
+    )
+    bias_keys = dot_tn(bias_blocks, bias_order)[:residues]
     turn = iota((tokens, tokens), 0)
     to_columns = one_hot(
         iota((tokens, tokens), 1) == (turn % sequences) * residues + turn // sequences
@@ -469,7 +462,7 @@
     values_in = alignment.astype(jnp.float32)
     normed_rows, scale_rows = normalize(values_in)
     normed_rows_low = normed_rows.astype(jnp.bfloat16)
-    row_gated, row_saved = attend(normed_rows_low, row_weights, bias_rows, residues)
+    row_gated, row_saved = attend(normed_rows_low, row_weights, bias_keys, residues)
     after_rows = (values_in + dot_nn(row_gated, row_output)).astype(jnp.bfloat16)
 
     column_weights = column_project_ref[...]
@@ -546,11 +539,13 @@
     for at in range(4):
         grad_row_project_ref[:, at, :] = raw[:, at * C : (at + 1) * C]
     bias_total = sum(part_rows(row_grad_scores, residues)) * (residues * sequences ** (-0.5))
-    bias_own = jnp.sum(
-        jnp.where(iota(bias_total.shape, 0) == own, bias_total, 0.0), axis=0, keepdims=True
-    )
+    bias_high = bias_total.astype(jnp.bfloat16)
+    bias_rest = (bias_total - bias_high.astype(jnp.float32)).astype(jnp.bfloat16)
+    shape = (H, lanes)
+    own_query = one_hot(iota(shape, 1) == iota(shape, 0) * residues + own)
+    bias_own = dot_nt(own_query, bias_high) + dot_nt(own_query, bias_rest)
     for at in range(H):
-        grad_bias_ref[at : at + 1, 0, :] = bias_own[:, at * residues : (at + 1) * residues]
+        grad_bias_ref[at : at + 1, 0, :] = bias_own[at : at + 1, :]
     grad_normed_rows = dot_nt(row_grad_proj[:residues], row_weights)
     grad_alignment_ref[0] = (
         grad_after_rows[:residues]

time: 29.8 us -> 26.9 us (0.903)
  Pallas kernels: 11.4 us -> 8.57 us
    pallas_call x1, Pallas kernels: 11.4 us -> 8.57 us  [gathered(): sample_call(daps, subs, residues, daps * subs, hidden_units)]
  transfers between devices with their start and end apart: 5 -> 5, of which waited for: 4 -> 4; matrix products, arithmetic and copies ran while one was open for 5% -> 6% of each run, Pallas kernels for 0% -> 0%
where the time goes in v3:
time: 26.9 us; the launch traced here: 26.7 us
  Pallas kernels  8.57 us (32%)
  starting transfers between devices  7.75 us (29%)
  waiting for transfers between devices  6.2 us (23%)
  other arithmetic  2.01 us (7%)
  local copies, waits for them, and re-layouts  1.46 us (5%)
  between operations  0.72 us (3%)
    pallas_call x1, Pallas kernels, gathered(): sample_call(daps, subs, residues, daps * subs, hidden_units)  8.57 us
    ppermute x3, starting transfers between devices, around(): blocks.append(lax.ppermute(values, axis, pairs))  6.09 us
    ppermute x2, waiting for transfers between devices, doubled(): return jnp.concatenate([values, lax.ppermute(values, axis, pairs)], axis=0)  4.3 us
    ppermute x3, waiting for transfers between devices, around(): blocks.append(lax.ppermute(values, axis, pairs))  1.9 us
    ppermute x2, starting transfers between devices, doubled(): return jnp.concatenate([values, lax.ppermute(values, axis, pairs)], axis=0)  1.66 us
    unnamed x9, local copies, waits for them, and re-layouts  1.46 us
    concatenate x1, other arithmetic, gathered(): jnp.concatenate([row_output, column_output, transition_out], axis=0)  1.15 us
    concatenate x1, other arithmetic, gathered(): block = jnp.concatenate([alignment, cotangent, bias_heads], axis=1)  0.79 us
  transfers between devices with their start and end apart: 5, of which 4 were waited for; matrix products, arithmetic and copies ran while one was open for 6% of the time, Pallas kernels for 0%

profile of v3, /device:TPU:0, one launch (start us, length us, event | category | flops | bytes accessed | tf_op | source)
XLA Modules:
  0.0 26.7 jit_solution(14340572169707796284)
XLA Ops:
  0.6 0.0 copy-start.1
  0.6 0.8 %fusion.1 = bf16[1,40,256]{2,1,0:T(8,128)(2,1)S(1)} fusion(bf16[1,8,16]{2,1,0:T(8,128)(2,1)} %bitcast.13, bf16[1,16,256]{2,1,0:T(8,128)(2,1)} %param.17, bf16[1,16,256]{2,1,0:T(8,128)(2,1)} %param.9), kind=kLoop, calls=%fused_computation.6 | loop fusion | flops 81920 | bytes 37120 | tf_op jit(solution)/shard_map/concatenate | solution.py:608
  1.4 0.0 copy-start.2
  1.4 5.1 %collective-permute-start.2 = (bf16[1,40,256]{2,1,0:T(8,128)(2,1)S(1)}, bf16[1,40,256]{2,1,0:T(8,128)(2,1)S(1)}, u32[]{:S(2)}, u32[]{:S(2)}) collective-permute-start(bf16[1,40,256]{2,1,0:T(8,128)(2,1)S(1)} %fusion.1), channel_id=1, source_target_pairs={{0,3},{1,0},{2,1},{3,2},{4,7},{5,4},{6,5},{7,6},{8,11},{9,8},{10,9... | collective-permute-start | bytes 61448 | tf_op jit(solution)/shard_map/ppermute | solution.py:583
  6.5 0.0 collective-permute-start.1
  6.5 1.0 %collective-permute-start = (bf16[1,40,256]{2,1,0:T(8,128)(2,1)S(1)}, bf16[1,40,256]{2,1,0:T(8,128)(2,1)S(1)}, u32[]{:S(2)}, u32[]{:S(2)}) collective-permute-start(bf16[1,40,256]{2,1,0:T(8,128)(2,1)S(1)} %fusion.1), channel_id=1, source_target_pairs={{0,1},{1,2},{2,3},{3,0},{4,5},{5,6},{6,7},{7,4},{8,9},{9,10},{10,1... | collective-permute-start | bytes 61448 | tf_op jit(solution)/shard_map/ppermute | solution.py:583
  7.5 1.2 %pad_maximum_fusion.refs_4_ = bf16[1536,256]{1,0:T(8,128)(2,1)S(1)} fusion(bf16[1024,256]{1,0:T(8,128)(2,1)} %param.16, bf16[256,256]{1,0:T(8,128)(2,1)} %param.14, bf16[256,256]{1,0:T(8,128)(2,1)} %param.12), kind=kLoop, calls=%fused_computation | loop fusion | flops 2359296 | bytes 1572864 | tf_op jit(solution)/shard_map/concatenate | solution.py:614
  8.7 0.0 copy-done.1
  8.7 0.0 copy-start
  8.7 0.1 copy.17
  8.8 0.0 copy-done.2
  8.8 0.1 copy.18
  8.9 1.0 %copy-done = bf16[256,2,1024]{2,1,0:T(2,128)(2,1)S(1)} copy-done((bf16[256,2,1024]{2,1,0:T(2,128)(2,1)S(1)}, bf16[256,2,1024]{2,1,0:T(2,128)(2,1)}, u32[]{:S(2)}) %copy-start) | copy-done | bytes 1048600
  9.9 0.3 copy.19
  10.2 0.0 collective-permute-done.2
  10.2 1.0 %collective-permute-done.1 = bf16[1,40,256]{2,1,0:T(8,128)(2,1)S(1)} collective-permute-done((bf16[1,40,256]{2,1,0:T(8,128)(2,1)S(1)}, bf16[1,40,256]{2,1,0:T(8,128)(2,1)S(1)}, u32[]{:S(2)}, u32[]{:S(2)}) %collective-permute-start.1) | collective-permute-done | bytes 20512 | tf_op jit(solution)/shard_map/ppermute | solution.py:583
  11.2 0.9 %collective-permute-done = bf16[1,40,256]{2,1,0:T(8,128)(2,1)S(1)} collective-permute-done((bf16[1,40,256]{2,1,0:T(8,128)(2,1)S(1)}, bf16[1,40,256]{2,1,0:T(8,128)(2,1)S(1)}, u32[]{:S(2)}, u32[]{:S(2)}) %collective-permute-start) | collective-permute-done | bytes 20512 | tf_op jit(solution)/shard_map/ppermute | solution.py:583
  12.1 1.6 %collective-permute-start.3 = (bf16[4,40,256]{2,1,0:T(8,128)(2,1)S(1)}, bf16[4,40,256]{2,1,0:T(8,128)(2,1)S(1)}, u32[]{:S(2)}, u32[]{:S(2)}) collective-permute-start(bf16[4,40,256]{2,1,0:T(8,128)(2,1)S(1)} %pad_maximum_fusion.3), channel_id=1, source_target_pairs={{0,8},{4,12},{8,0},{12,4},{1,9},{5,13},{9,1},{13,5},{2,10},{6,14},... | collective-permute-start | bytes 245768 | tf_op jit(solution)/shard_map/ppermute | solution.py:589
  13.7 2.9 %collective-permute-done.3 = bf16[4,40,256]{2,1,0:T(8,128)(2,1)S(1)} collective-permute-done((bf16[4,40,256]{2,1,0:T(8,128)(2,1)S(1)}, bf16[4,40,256]{2,1,0:T(8,128)(2,1)S(1)}, u32[]{:S(2)}, u32[]{:S(2)}) %collective-permute-start.3) | collective-permute-done | bytes 81952 | tf_op jit(solution)/shard_map/ppermute | solution.py:589
  16.6 0.1 collective-permute-start.4
  16.7 1.4 %collective-permute-done.4 = bf16[8,40,256]{2,1,0:T(8,128)(2,1)S(1)} collective-permute-done((bf16[8,40,256]{2,1,0:T(8,128)(2,1)S(1)}, bf16[8,40,256]{2,1,0:T(8,128)(2,1)S(1)}, u32[]{:S(2)}, u32[]{:S(2)}) %collective-permute-start.4) | collective-permute-done | bytes 163872 | tf_op jit(solution)/shard_map/ppermute | solution.py:589
  18.1 8.6 %sample.1 = (bf16[1,16,256]{2,1,0:T(8,128)(2,1)}, f32[8,1,16]{2,1,0:T(1,128)}, f32[16,4,256]{2,1,0:T(4,128)}, f32[16,256]{1,0:T(8,128)}, f32[16,4,256]{2,1,0:T(4...) custom-call(bf16[16,40,256]{2,1,0:T(8,128)(2,1)S(1)} %pad_maximum_fusion.1.refs_0_, ...), custom_call_target="tpu_custom_call" | custom-call | tf_op jit(solution)/shard_map/sample/pallas_call | solution.py:621
  (3 shorter events, 0.1 us)
Async XLA Ops:
  0.6 8.1 %copy-start.1 = (bf16[256,4,256]{2,1,0:T(4,128)(2,1)S(1)}, bf16[256,4,256]{2,1,0:T(4,128)(2,1)}, u32[]{:S(2)}) copy-start(bf16[256,4,256]{2,1,0:T(4,128)(2,1)} %param.11) | copy-start | bytes 1572868
  1.4 7.4 %copy-start.2 = (bf16[256,4,256]{2,1,0:T(4,128)(2,1)S(1)}, bf16[256,4,256]{2,1,0:T(4,128)(2,1)}, u32[]{:S(2)}) copy-start(bf16[256,4,256]{2,1,0:T(4,128)(2,1)} %param.13) | copy-start | bytes 1572868
  1.4 8.8 %collective-permute-start.2 = (bf16[1,40,256]{2,1,0:T(8,128)(2,1)S(1)}, bf16[1,40,256]{2,1,0:T(8,128)(2,1)S(1)}, u32[]{:S(2)}, u32[]{:S(2)}) collective-permute-start(bf16[1,40,256]{2,1,0:T(8,128)(2,1)S(1)} %fusion.1), channel_id=1, source_target_pairs={{0,3},{1,0},{2,1},{3,2},{4,7},{5,4},{6,5},{7,6},{8,11},{9,8},{10,9... | collective-permute-start | bytes 61448 | tf_op jit(solution)/shard_map/ppermute | solution.py:583
  6.5 4.7 %collective-permute-start.1 = (bf16[1,40,256]{2,1,0:T(8,128)(2,1)S(1)}, bf16[1,40,256]{2,1,0:T(8,128)(2,1)S(1)}, u32[]{:S(2)}, u32[]{:S(2)}) collective-permute-start(bf16[1,40,256]{2,1,0:T(8,128)(2,1)S(1)} %fusion.1), channel_id=1, source_target_pairs={{0,2},{1,3},{2,0},{3,1},{4,6},{5,7},{6,4},{7,5},{8,10},{9,11},{10,... | collective-permute-start | bytes 61448 | tf_op jit(solution)/shard_map/ppermute | solution.py:583
  6.5 5.6 %collective-permute-start = (bf16[1,40,256]{2,1,0:T(8,128)(2,1)S(1)}, bf16[1,40,256]{2,1,0:T(8,128)(2,1)S(1)}, u32[]{:S(2)}, u32[]{:S(2)}) collective-permute-start(bf16[1,40,256]{2,1,0:T(8,128)(2,1)S(1)} %fusion.1), channel_id=1, source_target_pairs={{0,1},{1,2},{2,3},{3,0},{4,5},{5,6},{6,7},{7,4},{8,9},{9,10},{10,1... | collective-permute-start | bytes 61448 | tf_op jit(solution)/shard_map/ppermute | solution.py:583
  8.7 1.2 %copy-start = (bf16[256,2,1024]{2,1,0:T(2,128)(2,1)S(1)}, bf16[256,2,1024]{2,1,0:T(2,128)(2,1)}, u32[]{:S(2)}) copy-start(bf16[256,2,1024]{2,1,0:T(2,128)(2,1)} %param.15) | copy-start | bytes 3145732
  12.1 4.5 %collective-permute-start.3 = (bf16[4,40,256]{2,1,0:T(8,128)(2,1)S(1)}, bf16[4,40,256]{2,1,0:T(8,128)(2,1)S(1)}, u32[]{:S(2)}, u32[]{:S(2)}) collective-permute-start(bf16[4,40,256]{2,1,0:T(8,128)(2,1)S(1)} %pad_maximum_fusion.3), channel_id=1, source_target_pairs={{0,8},{4,12},{8,0},{12,4},{1,9},{5,13},{9,1},{13,5},{2,10},{6,14},... | collective-permute-start | bytes 245768 | tf_op jit(solution)/shard_map/ppermute | solution.py:589
  16.6 1.5 %collective-permute-start.4 = (bf16[8,40,256]{2,1,0:T(8,128)(2,1)S(1)}, bf16[8,40,256]{2,1,0:T(8,128)(2,1)S(1)}, u32[]{:S(2)}, u32[]{:S(2)}) collective-permute-start(bf16[8,40,256]{2,1,0:T(8,128)(2,1)S(1)} %pad_maximum_fusion.2), channel_id=1, source_target_pairs={{0,4},{4,0},{8,12},{12,8},{1,5},{5,1},{9,13},{13,9},{2,6},{6,2},{1... | collective-permute-start | bytes 491528 | tf_op jit(solution)/shard_map/ppermute | solution.py:589

commit v4 on v3

--- a/solution.py
+++ b/solution.py
@@ -308,18 +308,43 @@
     return values.reshape(values.shape[0] // length, length, values.shape[1])
 
 
+def part_of(values, size):
+    return lax.shift_right_logical(values, jnp.full_like(values, size.bit_length() - 1))
+
+
+def place_in(values, size):
+    return values & (size - 1)
+
+
+LANES = 128
+TILE_HEADS = LANES // DH
+
+
 def by_head(rows, length):
-    tall = jnp.concatenate([rows] * H, axis=0)
-    own = iota(tall.shape, 0) // length == iota(tall.shape, 1) // DH
-    return jnp.where(own, tall, jnp.zeros_like(tall))
-
-
-def from_heads(tall, length):
-    head = iota((length, tall.shape[1]), 1) // DH
-    kept = tall[:length]
-    for at in range(1, H):
-        kept = jnp.where(head == at, tall[at * length : (at + 1) * length], kept)
-    return kept
+    head = part_of(iota((length, LANES), 1), DH)
+    none = jnp.zeros((length, LANES), rows.dtype)
+    tall = []
+    for at in range(H):
+        own = at // TILE_HEADS
+        tile = rows[:, own * LANES : (own + 1) * LANES]
+        tile = jnp.where(head == at % TILE_HEADS, tile, none)
+        tiles = [tile if other == own else none for other in range(H // TILE_HEADS)]
+        tall.append(jnp.concatenate(tiles, axis=1))
+    return jnp.concatenate(tall, axis=0)
+
+
+def turned_product(former, latter, length):
+    turned = jnp.transpose(former)
+    head = part_of(iota((length, LANES), 1), DH)
+    tiles = []
+    for at in range(H // TILE_HEADS):
+        rows = turned[at * TILE_HEADS * length : (at + 1) * TILE_HEADS * length]
+        tall = dot_nn(rows, latter[:, at * LANES : (at + 1) * LANES])
+        kept = tall[:length]
+        for other in range(1, TILE_HEADS):
+            kept = jnp.where(head == other, tall[other * length : (other + 1) * length], kept)
+        tiles.append(kept)
+    return jnp.concatenate(tiles, axis=1)
 
 
 def part_rows(values, length):
@@ -348,7 +373,7 @@
     shares_low = shares.astype(jnp.bfloat16)
     blended = jnp.concatenate(
         [
-            from_heads(dot_tn(share, value), length)
+            turned_product(share, value, length)
             for share, value in zip(part_rows(shares_low, length), part_rows(values, length))
         ],
         axis=0,
@@ -379,7 +404,7 @@
     for score, key, query in zip(
         part_rows(grad_low, length), part_rows(key_rows, length), part_rows(queries, length)
     ):
-        grad_queries.append(from_heads(dot_tn(score, key), length))
+        grad_queries.append(turned_product(score, key, length))
         grad_keys.append(dot_nn(score, by_head(query, length)))
     grad_gate = grad_gated * blended * gating * (1.0 - gating)
     grad_proj = jnp.concatenate(
@@ -432,26 +457,25 @@
     bias_blocks = gathered_ref[:, 2 * residues :, :lanes].astype(jnp.float32)
     bias_blocks = bias_blocks.reshape(sequences * H, lanes).astype(jnp.bfloat16)
     block_at = iota((sequences * H, lanes), 0)
-    from_place = block_at // H
-    from_turn = from_place // subs
+    from_place = part_of(block_at, H)
+    from_turn = part_of(from_place, subs)
     from_dap = jnp.zeros_like(from_place)
     mask = 1
     while mask < daps:
-        turned = from_turn // (daps // (2 * mask)) % 2
+        turned = place_in(part_of(from_turn, daps // (2 * mask)), 2)
         kept = lax.rem(dap // mask, 2)
         from_dap = from_dap + mask * jnp.where(turned == 1, 1 - kept, kept)
         mask *= 2
-    from_sub = sub - from_place % subs
-    from_sub = jnp.where(from_sub < 0, from_sub + subs, from_sub)
+    from_sub = place_in(sub + from_place, subs)
     query_lane = iota(block_at.shape, 1)
     bias_order = one_hot(
-        (from_dap * subs + from_sub == query_lane % residues)
-        & (block_at % H == query_lane // residues)
+        (from_dap * subs + from_sub == place_in(query_lane, residues))
+        & (place_in(block_at, H) == part_of(query_lane, residues))
     )
     bias_keys = dot_tn(bias_blocks, bias_order)[:residues]
     turn = iota((tokens, tokens), 0)
     to_columns = one_hot(
-        iota((tokens, tokens), 1) == (turn % sequences) * residues + turn // sequences
+        iota((tokens, tokens), 1) == place_in(turn, sequences) * residues + part_of(turn, sequences)
     )
 
     row_output = outputs_ref[: H * DH, :]
@@ -579,7 +603,7 @@
     size = lax.axis_size(axis)
     blocks = [values]
     for shift in range(1, size):
-        pairs = [(source, (source + shift) % size) for source in range(size)]
+        pairs = [(source, (source - shift) % size) for source in range(size)]
         blocks.append(lax.ppermute(values, axis, pairs))
     return jnp.concatenate(blocks, axis=0)
 

time: 26.9 us -> 25.9 us (0.963)
  waiting for transfers between devices: 6.2 us -> 4.31 us
  starting transfers between devices: 7.75 us -> 8.65 us
    ppermute x3, waiting for transfers between devices: 1.9 us -> 0.01 us  [around(): blocks.append(lax.ppermute(values, axis, pairs))]
    ppermute x3, starting transfers between devices: 6.09 us -> 6.99 us  [around(): blocks.append(lax.ppermute(values, axis, pairs))]
  transfers between devices with their start and end apart: 5 -> 5, of which waited for: 4 -> 2; matrix products, arithmetic and copies ran while one was open for 6% -> 6% of each run, Pallas kernels for 0% -> 0%
where the time goes in v4:
time: 25.9 us; the launch traced here: 25.7 us
  starting transfers between devices  8.65 us (33%)
  Pallas kernels  8.55 us (33%)
  waiting for transfers between devices  4.31 us (17%)
  other arithmetic  2.01 us (8%)
  local copies, waits for them, and re-layouts  1.46 us (6%)
  between operations  0.74 us (3%)
    pallas_call x1, Pallas kernels, gathered(): sample_call(daps, subs, residues, daps * subs, hidden_units)  8.55 us
    ppermute x3, starting transfers between devices, around(): blocks.append(lax.ppermute(values, axis, pairs))  6.99 us
    ppermute x2, waiting for transfers between devices, doubled(): return jnp.concatenate([values, lax.ppermute(values, axis, pairs)], axis=0)  4.3 us
    ppermute x2, starting transfers between devices, doubled(): return jnp.concatenate([values, lax.ppermute(values, axis, pairs)], axis=0)  1.66 us
    unnamed x9, local copies, waits for them, and re-layouts  1.46 us
    concatenate x1, other arithmetic, gathered(): jnp.concatenate([row_output, column_output, transition_out], axis=0)  1.15 us
    concatenate x1, other arithmetic, gathered(): block = jnp.concatenate([alignment, cotangent, bias_heads], axis=1)  0.79 us
  transfers between devices with their start and end apart: 5, of which 2 were waited for; matrix products, arithmetic and copies ran while one was open for 6% of the time, Pallas kernels for 0%

profile of v4, /device:TPU:0, one launch (start us, length us, event | category | flops | bytes accessed | tf_op | source)
XLA Modules:
  0.0 25.7 jit_solution(1076897676292685092)
XLA Ops:
  0.6 0.0 copy-start.1
  0.6 0.8 %fusion.1 = bf16[1,40,256]{2,1,0:T(8,128)(2,1)S(1)} fusion(bf16[1,8,16]{2,1,0:T(8,128)(2,1)} %bitcast.13, bf16[1,16,256]{2,1,0:T(8,128)(2,1)} %param.17, bf16[1,16,256]{2,1,0:T(8,128)(2,1)} %param.9), kind=kLoop, calls=%fused_computation.6 | loop fusion | flops 81920 | bytes 37120 | tf_op jit(solution)/shard_map/concatenate | solution.py:632
  1.4 0.0 copy-start.2
  1.4 3.1 %collective-permute-start.2 = (bf16[1,40,256]{2,1,0:T(8,128)(2,1)S(1)}, bf16[1,40,256]{2,1,0:T(8,128)(2,1)S(1)}, u32[]{:S(2)}, u32[]{:S(2)}) collective-permute-start(bf16[1,40,256]{2,1,0:T(8,128)(2,1)S(1)} %fusion.1), channel_id=1, source_target_pairs={{0,1},{1,2},{2,3},{3,0},{4,5},{5,6},{6,7},{7,4},{8,9},{9,10},{10,1... | collective-permute-start | bytes 61448 | tf_op jit(solution)/shard_map/ppermute | solution.py:607
  4.5 2.6 %collective-permute-start.1 = (bf16[1,40,256]{2,1,0:T(8,128)(2,1)S(1)}, bf16[1,40,256]{2,1,0:T(8,128)(2,1)S(1)}, u32[]{:S(2)}, u32[]{:S(2)}) collective-permute-start(bf16[1,40,256]{2,1,0:T(8,128)(2,1)S(1)} %fusion.1), channel_id=1, source_target_pairs={{0,2},{1,3},{2,0},{3,1},{4,6},{5,7},{6,4},{7,5},{8,10},{9,11},{10,... | collective-permute-start | bytes 61448 | tf_op jit(solution)/shard_map/ppermute | solution.py:607
  7.1 1.3 %collective-permute-start = (bf16[1,40,256]{2,1,0:T(8,128)(2,1)S(1)}, bf16[1,40,256]{2,1,0:T(8,128)(2,1)S(1)}, u32[]{:S(2)}, u32[]{:S(2)}) collective-permute-start(bf16[1,40,256]{2,1,0:T(8,128)(2,1)S(1)} %fusion.1), channel_id=1, source_target_pairs={{0,3},{1,0},{2,1},{3,2},{4,7},{5,4},{6,5},{7,6},{8,11},{9,8},{10,9... | collective-permute-start | bytes 61448 | tf_op jit(solution)/shard_map/ppermute | solution.py:607
  8.4 1.2 %pad_maximum_fusion.refs_4_ = bf16[1536,256]{1,0:T(8,128)(2,1)S(1)} fusion(bf16[1024,256]{1,0:T(8,128)(2,1)} %param.16, bf16[256,256]{1,0:T(8,128)(2,1)} %param.14, bf16[256,256]{1,0:T(8,128)(2,1)} %param.12), kind=kLoop, calls=%fused_computation | loop fusion | flops 2359296 | bytes 1572864 | tf_op jit(solution)/shard_map/concatenate | solution.py:638
  9.6 0.0 copy-done.1
  9.6 0.0 copy-start
  9.6 0.1 copy.17
  9.7 0.0 copy-done.2
  9.7 0.1 copy.18
  9.8 1.0 %copy-done = bf16[256,2,1024]{2,1,0:T(2,128)(2,1)S(1)} copy-done((bf16[256,2,1024]{2,1,0:T(2,128)(2,1)S(1)}, bf16[256,2,1024]{2,1,0:T(2,128)(2,1)}, u32[]{:S(2)}) %copy-start) | copy-done | bytes 1048600
  10.8 0.3 %copy.19 = bf16[32,8,2,1024]{3,1,2,0:T(8,128)(2,1)S(1)} copy(bf16[32,8,2,1024]{3,2,1,0:T(2,128)(2,1)S(1)} %bitcast.10) | data formatting | bytes 2097152
  11.1 0.0 collective-permute-done.2
  11.1 0.0 collective-permute-done.1
  11.1 0.0 collective-permute-done
  11.1 1.6 %collective-permute-start.3 = (bf16[4,40,256]{2,1,0:T(8,128)(2,1)S(1)}, bf16[4,40,256]{2,1,0:T(8,128)(2,1)S(1)}, u32[]{:S(2)}, u32[]{:S(2)}) collective-permute-start(bf16[4,40,256]{2,1,0:T(8,128)(2,1)S(1)} %pad_maximum_fusion.3), channel_id=1, source_target_pairs={{0,8},{4,12},{8,0},{12,4},{1,9},{5,13},{9,1},{13,5},{2,10},{6,14},... | collective-permute-start | bytes 245768 | tf_op jit(solution)/shard_map/ppermute | solution.py:613
  12.7 2.9 %collective-permute-done.3 = bf16[4,40,256]{2,1,0:T(8,128)(2,1)S(1)} collective-permute-done((bf16[4,40,256]{2,1,0:T(8,128)(2,1)S(1)}, bf16[4,40,256]{2,1,0:T(8,128)(2,1)S(1)}, u32[]{:S(2)}, u32[]{:S(2)}) %collective-permute-start.3) | collective-permute-done | bytes 81952 | tf_op jit(solution)/shard_map/ppermute | solution.py:613
  15.7 0.1 collective-permute-start.4
  15.8 1.4 %collective-permute-done.4 = bf16[8,40,256]{2,1,0:T(8,128)(2,1)S(1)} collective-permute-done((bf16[8,40,256]{2,1,0:T(8,128)(2,1)S(1)}, bf16[8,40,256]{2,1,0:T(8,128)(2,1)S(1)}, u32[]{:S(2)}, u32[]{:S(2)}) %collective-permute-start.4) | collective-permute-done | bytes 163872 | tf_op jit(solution)/shard_map/ppermute | solution.py:613
  17.2 8.6 %sample.1 = (bf16[1,16,256]{2,1,0:T(8,128)(2,1)}, f32[8,1,16]{2,1,0:T(1,128)}, f32[16,4,256]{2,1,0:T(4,128)}, f32[16,256]{1,0:T(8,128)}, f32[16,4,256]{2,1,0:T(4...) custom-call(bf16[16,40,256]{2,1,0:T(8,128)(2,1)S(1)} %pad_maximum_fusion.1.refs_0_, ...), custom_call_target="tpu_custom_call" | custom-call | tf_op jit(solution)/shard_map/sample/pallas_call | solution.py:645
  (3 shorter events, 0.1 us)
Async XLA Ops:
  0.6 9.0 %copy-start.1 = (bf16[256,4,256]{2,1,0:T(4,128)(2,1)S(1)}, bf16[256,4,256]{2,1,0:T(4,128)(2,1)}, u32[]{:S(2)}) copy-start(bf16[256,4,256]{2,1,0:T(4,128)(2,1)} %param.11) | copy-start | bytes 1572868
  1.4 8.3 %copy-start.2 = (bf16[256,4,256]{2,1,0:T(4,128)(2,1)S(1)}, bf16[256,4,256]{2,1,0:T(4,128)(2,1)}, u32[]{:S(2)}) copy-start(bf16[256,4,256]{2,1,0:T(4,128)(2,1)} %param.13) | copy-start | bytes 1572868
  1.4 9.7 %collective-permute-start.2 = (bf16[1,40,256]{2,1,0:T(8,128)(2,1)S(1)}, bf16[1,40,256]{2,1,0:T(8,128)(2,1)S(1)}, u32[]{:S(2)}, u32[]{:S(2)}) collective-permute-start(bf16[1,40,256]{2,1,0:T(8,128)(2,1)S(1)} %fusion.1), channel_id=1, source_target_pairs={{0,1},{1,2},{2,3},{3,0},{4,5},{5,6},{6,7},{7,4},{8,9},{9,10},{10,1... | collective-permute-start | bytes 61448 | tf_op jit(solution)/shard_map/ppermute | solution.py:607
  4.5 6.6 %collective-permute-start.1 = (bf16[1,40,256]{2,1,0:T(8,128)(2,1)S(1)}, bf16[1,40,256]{2,1,0:T(8,128)(2,1)S(1)}, u32[]{:S(2)}, u32[]{:S(2)}) collective-permute-start(bf16[1,40,256]{2,1,0:T(8,128)(2,1)S(1)} %fusion.1), channel_id=1, source_target_pairs={{0,2},{1,3},{2,0},{3,1},{4,6},{5,7},{6,4},{7,5},{8,10},{9,11},{10,... | collective-permute-start | bytes 61448 | tf_op jit(solution)/shard_map/ppermute | solution.py:607
  7.1 4.0 %collective-permute-start = (bf16[1,40,256]{2,1,0:T(8,128)(2,1)S(1)}, bf16[1,40,256]{2,1,0:T(8,128)(2,1)S(1)}, u32[]{:S(2)}, u32[]{:S(2)}) collective-permute-start(bf16[1,40,256]{2,1,0:T(8,128)(2,1)S(1)} %fusion.1), channel_id=1, source_target_pairs={{0,3},{1,0},{2,1},{3,2},{4,7},{5,4},{6,5},{7,6},{8,11},{9,8},{10,9... | collective-permute-start | bytes 61448 | tf_op jit(solution)/shard_map/ppermute | solution.py:607
  9.6 1.2 %copy-start = (bf16[256,2,1024]{2,1,0:T(2,128)(2,1)S(1)}, bf16[256,2,1024]{2,1,0:T(2,128)(2,1)}, u32[]{:S(2)}) copy-start(bf16[256,2,1024]{2,1,0:T(2,128)(2,1)} %param.15) | copy-start | bytes 3145732
  11.1 4.5 %collective-permute-start.3 = (bf16[4,40,256]{2,1,0:T(8,128)(2,1)S(1)}, bf16[4,40,256]{2,1,0:T(8,128)(2,1)S(1)}, u32[]{:S(2)}, u32[]{:S(2)}) collective-permute-start(bf16[4,40,256]{2,1,0:T(8,128)(2,1)S(1)} %pad_maximum_fusion.3), channel_id=1, source_target_pairs={{0,8},{4,12},{8,0},{12,4},{1,9},{5,13},{9,1},{13,5},{2,10},{6,14},... | collective-permute-start | bytes 245768 | tf_op jit(solution)/shard_map/ppermute | solution.py:613
  15.7 1.5 %collective-permute-start.4 = (bf16[8,40,256]{2,1,0:T(8,128)(2,1)S(1)}, bf16[8,40,256]{2,1,0:T(8,128)(2,1)S(1)}, u32[]{:S(2)}, u32[]{:S(2)}) collective-permute-start(bf16[8,40,256]{2,1,0:T(8,128)(2,1)S(1)} %pad_maximum_fusion.2), channel_id=1, source_target_pairs={{0,4},{4,0},{8,12},{12,8},{1,5},{5,1},{9,13},{13,9},{2,6},{6,2},{1... | collective-permute-start | bytes 491528 | tf_op jit(solution)/shard_map/ppermute | solution.py:613

commit v5 on v4

--- a/solution.py
+++ b/solution.py
@@ -631,18 +631,19 @@
     bias_heads = jnp.pad(jnp.swapaxes(pair_bias, 0, 1), ((0, 0), (0, 0), (0, C - residues)))
     block = jnp.concatenate([alignment, cotangent, bias_heads], axis=1)
     blocks = around(lax.optimization_barrier(block), "sub")
-    weights = (
-        row_project.reshape(C, 4 * H * DH),
-        column_project.reshape(C, 4 * H * DH),
+    early = (row_project.reshape(C, 4 * H * DH), column_project.reshape(C, 4 * H * DH))
+    late = (
         transition_in.reshape(C, 2 * hidden_units),
         jnp.concatenate([row_output, column_output, transition_out], axis=0),
     )
-    blocks, weights = lax.optimization_barrier((blocks, weights))
+    blocks, early = lax.optimization_barrier((blocks, early))
     mask = daps // 2
     while mask:
         blocks = doubled(blocks, "dap", mask)
+        if mask > 1:
+            blocks, late = lax.optimization_barrier((blocks, late))
         mask //= 2
-    return sample_call(daps, subs, residues, daps * subs, hidden_units)(blocks, *weights)
+    return sample_call(daps, subs, residues, daps * subs, hidden_units)(blocks, *early, *late)
 
 
 def gathered_fits(alignment, transition_out):

time: 25.9 us -> 25.7 us (level)
  other arithmetic: 2.01 us -> 0.9 us
  waiting for transfers between devices: 4.31 us -> 5.03 us
    concatenate x1, other arithmetic: 1.15 us -> 0.05 us  [gathered(): jnp.concatenate([row_output, column_output, transition_out], axis=0)]
    ppermute x3, waiting for transfers between devices: 0.01 us -> 1.08 us  [around(): blocks.append(lax.ppermute(values, axis, pairs))]
    ppermute x2, waiting for transfers between devices: 4.3 us -> 3.96 us  [doubled(): return jnp.concatenate([values, lax.ppermute(values, axis, pairs)], axis=0)]
    unnamed x9 -> x13, local copies, waits for them, and re-layouts: 1.46 us -> 1.58 us
  transfers between devices with their start and end apart: 5 -> 5, of which waited for: 2 -> 3; matrix products, arithmetic and copies ran while one was open for 6% -> 6% of each run, Pallas kernels for 0% -> 0%
where the time goes in v5:
time: 25.7 us; the launch traced here: 25.4 us
  starting transfers between devices  8.65 us (34%)
  Pallas kernels  8.55 us (33%)
  waiting for transfers between devices  5.03 us (20%)
  local copies, waits for them, and re-layouts  1.58 us (6%)
  other arithmetic  0.9 us (4%)
  between operations  0.74 us (3%)
    pallas_call x1, Pallas kernels, gathered(): sample_call(daps, subs, residues, daps * subs, hidden_units)  8.55 us
    ppermute x3, starting transfers between devices, around(): blocks.append(lax.ppermute(values, axis, pairs))  6.99 us
    ppermute x2, waiting for transfers between devices, doubled(): return jnp.concatenate([values, lax.ppermute(values, axis, pairs)], axis=0)  3.96 us
    ppermute x2, starting transfers between devices, doubled(): return jnp.concatenate([values, lax.ppermute(values, axis, pairs)], axis=0)  1.66 us
    unnamed x13, local copies, waits for them, and re-layouts  1.58 us
    ppermute x3, waiting for transfers between devices, around(): blocks.append(lax.ppermute(values, axis, pairs))  1.08 us
    concatenate x1, other arithmetic, gathered(): block = jnp.concatenate([alignment, cotangent, bias_heads], axis=1)  0.79 us
  transfers between devices with their start and end apart: 5, of which 3 were waited for; matrix products, arithmetic and copies ran while one was open for 6% of the time, Pallas kernels for 0%

profile of v5, /device:TPU:0, one launch (start us, length us, event | category | flops | bytes accessed | tf_op | source)
XLA Modules:
  0.0 25.4 jit_solution(11830154191766603685)
XLA Ops:
  0.6 0.0 copy-start.2
  0.6 0.8 %fusion.1 = bf16[1,40,256]{2,1,0:T(8,128)(2,1)S(1)} fusion(bf16[1,8,16]{2,1,0:T(8,128)(2,1)} %bitcast.13, bf16[1,16,256]{2,1,0:T(8,128)(2,1)} %param.17, bf16[1,16,256]{2,1,0:T(8,128)(2,1)} %param.9), kind=kLoop, calls=%fused_computation.6 | loop fusion | flops 81920 | bytes 37120 | tf_op jit(solution)/shard_map/concatenate | solution.py:632
  1.4 3.1 %collective-permute-start.2 = (bf16[1,40,256]{2,1,0:T(8,128)(2,1)S(1)}, bf16[1,40,256]{2,1,0:T(8,128)(2,1)S(1)}, u32[]{:S(2)}, u32[]{:S(2)}) collective-permute-start(bf16[1,40,256]{2,1,0:T(8,128)(2,1)S(1)} %fusion.1), channel_id=1, source_target_pairs={{0,1},{1,2},{2,3},{3,0},{4,5},{5,6},{6,7},{7,4},{8,9},{9,10},{10,1... | collective-permute-start | bytes 61448 | tf_op jit(solution)/shard_map/ppermute | solution.py:607
  4.5 2.6 %collective-permute-start.1 = (bf16[1,40,256]{2,1,0:T(8,128)(2,1)S(1)}, bf16[1,40,256]{2,1,0:T(8,128)(2,1)S(1)}, u32[]{:S(2)}, u32[]{:S(2)}) collective-permute-start(bf16[1,40,256]{2,1,0:T(8,128)(2,1)S(1)} %fusion.1), channel_id=1, source_target_pairs={{0,2},{1,3},{2,0},{3,1},{4,6},{5,7},{6,4},{7,5},{8,10},{9,11},{10,... | collective-permute-start | bytes 61448 | tf_op jit(solution)/shard_map/ppermute | solution.py:607
  7.1 1.3 %collective-permute-start = (bf16[1,40,256]{2,1,0:T(8,128)(2,1)S(1)}, bf16[1,40,256]{2,1,0:T(8,128)(2,1)S(1)}, u32[]{:S(2)}, u32[]{:S(2)}) collective-permute-start(bf16[1,40,256]{2,1,0:T(8,128)(2,1)S(1)} %fusion.1), channel_id=1, source_target_pairs={{0,3},{1,0},{2,1},{3,2},{4,7},{5,4},{6,5},{7,6},{8,11},{9,8},{10,9... | collective-permute-start | bytes 61448 | tf_op jit(solution)/shard_map/ppermute | solution.py:607
  8.4 0.0 copy-start.1
  8.4 0.0 copy-start.3
  8.4 0.0 copy-start.4
  8.4 1.2 %copy.17 = bf16[32,8,4,256]{3,1,2,0:T(8,128)(2,1)S(1)} copy(bf16[32,8,4,256]{3,2,1,0:T(4,128)(2,1)} %bitcast.11) | data formatting | bytes 1048576
  9.6 0.0 copy-done.2
  9.7 0.1 copy.18
  9.8 0.0 copy-start
  9.8 0.0 collective-permute-done.2
  9.8 0.0 collective-permute-done.1
  9.8 1.1 %collective-permute-done = bf16[1,40,256]{2,1,0:T(8,128)(2,1)S(1)} collective-permute-done((bf16[1,40,256]{2,1,0:T(8,128)(2,1)S(1)}, bf16[1,40,256]{2,1,0:T(8,128)(2,1)S(1)}, u32[]{:S(2)}, u32[]{:S(2)}) %collective-permute-start) | collective-permute-done | bytes 20512 | tf_op jit(solution)/shard_map/ppermute | solution.py:607
  10.9 1.6 %collective-permute-start.3 = (bf16[4,40,256]{2,1,0:T(8,128)(2,1)S(1)}, bf16[4,40,256]{2,1,0:T(8,128)(2,1)S(1)}, u32[]{:S(2)}, u32[]{:S(2)}) collective-permute-start(bf16[4,40,256]{2,1,0:T(8,128)(2,1)S(1)} %pad_maximum_fusion.3), channel_id=1, source_target_pairs={{0,8},{4,12},{8,0},{12,4},{1,9},{5,13},{9,1},{13,5},{2,10},{6,14},... | collective-permute-start | bytes 245768 | tf_op jit(solution)/shard_map/ppermute | solution.py:613
  12.5 0.0 copy-done.1
  12.5 0.0 copy-done.3
  12.5 0.0 copy-done.4
  12.5 0.1 pad_maximum_fusion.refs_4_
  12.5 0.0 copy-done
  12.5 0.3 %copy.19 = bf16[32,8,2,1024]{3,1,2,0:T(8,128)(2,1)S(1)} copy(bf16[32,8,2,1024]{3,2,1,0:T(2,128)(2,1)S(1)} %bitcast.10) | data formatting | bytes 2097152
  12.8 2.6 %collective-permute-done.3 = bf16[4,40,256]{2,1,0:T(8,128)(2,1)S(1)} collective-permute-done((bf16[4,40,256]{2,1,0:T(8,128)(2,1)S(1)}, bf16[4,40,256]{2,1,0:T(8,128)(2,1)S(1)}, u32[]{:S(2)}, u32[]{:S(2)}) %collective-permute-start.3) | collective-permute-done | bytes 81952 | tf_op jit(solution)/shard_map/ppermute | solution.py:613
  15.4 0.1 collective-permute-start.4
  15.5 1.4 %collective-permute-done.4 = bf16[8,40,256]{2,1,0:T(8,128)(2,1)S(1)} collective-permute-done((bf16[8,40,256]{2,1,0:T(8,128)(2,1)S(1)}, bf16[8,40,256]{2,1,0:T(8,128)(2,1)S(1)}, u32[]{:S(2)}, u32[]{:S(2)}) %collective-permute-start.4) | collective-permute-done | bytes 163872 | tf_op jit(solution)/shard_map/ppermute | solution.py:613
  16.9 8.5 %sample.1 = (bf16[1,16,256]{2,1,0:T(8,128)(2,1)}, f32[8,1,16]{2,1,0:T(1,128)}, f32[16,4,256]{2,1,0:T(4,128)}, f32[16,256]{1,0:T(8,128)}, f32[16,4,256]{2,1,0:T(4...) custom-call(bf16[16,40,256]{2,1,0:T(8,128)(2,1)S(1)} %pad_maximum_fusion.1.refs_0_, ...), custom_call_target="tpu_custom_call" | custom-call | tf_op jit(solution)/shard_map/sample/pallas_call | solution.py:646
  (3 shorter events, 0.1 us)
Async XLA Ops:
  0.6 9.0 %copy-start.2 = (bf16[256,4,256]{2,1,0:T(4,128)(2,1)S(1)}, bf16[256,4,256]{2,1,0:T(4,128)(2,1)}, u32[]{:S(2)}) copy-start(bf16[256,4,256]{2,1,0:T(4,128)(2,1)} %param.13) | copy-start | bytes 1572868
  1.4 8.3 %collective-permute-start.2 = (bf16[1,40,256]{2,1,0:T(8,128)(2,1)S(1)}, bf16[1,40,256]{2,1,0:T(8,128)(2,1)S(1)}, u32[]{:S(2)}, u32[]{:S(2)}) collective-permute-start(bf16[1,40,256]{2,1,0:T(8,128)(2,1)S(1)} %fusion.1), channel_id=1, source_target_pairs={{0,1},{1,2},{2,3},{3,0},{4,5},{5,6},{6,7},{7,4},{8,9},{9,10},{10,1... | collective-permute-start | bytes 61448 | tf_op jit(solution)/shard_map/ppermute | solution.py:607
  4.5 5.3 %collective-permute-start.1 = (bf16[1,40,256]{2,1,0:T(8,128)(2,1)S(1)}, bf16[1,40,256]{2,1,0:T(8,128)(2,1)S(1)}, u32[]{:S(2)}, u32[]{:S(2)}) collective-permute-start(bf16[1,40,256]{2,1,0:T(8,128)(2,1)S(1)} %fusion.1), channel_id=1, source_target_pairs={{0,2},{1,3},{2,0},{3,1},{4,6},{5,7},{6,4},{7,5},{8,10},{9,11},{10,... | collective-permute-start | bytes 61448 | tf_op jit(solution)/shard_map/ppermute | solution.py:607
  7.1 3.8 %collective-permute-start = (bf16[1,40,256]{2,1,0:T(8,128)(2,1)S(1)}, bf16[1,40,256]{2,1,0:T(8,128)(2,1)S(1)}, u32[]{:S(2)}, u32[]{:S(2)}) collective-permute-start(bf16[1,40,256]{2,1,0:T(8,128)(2,1)S(1)} %fusion.1), channel_id=1, source_target_pairs={{0,3},{1,0},{2,1},{3,2},{4,7},{5,4},{6,5},{7,6},{8,11},{9,8},{10,9... | collective-permute-start | bytes 61448 | tf_op jit(solution)/shard_map/ppermute | solution.py:607
  8.4 4.0 %copy-start.1 = (bf16[1024,256]{1,0:T(8,128)(2,1)S(1)}, bf16[1024,256]{1,0:T(8,128)(2,1)}, u32[]{:S(2)}) copy-start(bf16[1024,256]{1,0:T(8,128)(2,1)} %param.16) | copy-start | bytes 1572868
  8.4 4.0 %copy-start.3 = (bf16[256,256]{1,0:T(8,128)(2,1)S(1)}, bf16[256,256]{1,0:T(8,128)(2,1)}, u32[]{:S(2)}) copy-start(bf16[256,256]{1,0:T(8,128)(2,1)} %param.14) | copy-start | bytes 393220
  8.4 4.0 %copy-start.4 = (bf16[256,256]{1,0:T(8,128)(2,1)S(1)}, bf16[256,256]{1,0:T(8,128)(2,1)}, u32[]{:S(2)}) copy-start(bf16[256,256]{1,0:T(8,128)(2,1)} %param.12) | copy-start | bytes 393220
  9.8 2.8 %copy-start = (bf16[256,2,1024]{2,1,0:T(2,128)(2,1)S(1)}, bf16[256,2,1024]{2,1,0:T(2,128)(2,1)}, u32[]{:S(2)}) copy-start(bf16[256,2,1024]{2,1,0:T(2,128)(2,1)} %param.15) | copy-start | bytes 3145732
  10.9 4.5 %collective-permute-start.3 = (bf16[4,40,256]{2,1,0:T(8,128)(2,1)S(1)}, bf16[4,40,256]{2,1,0:T(8,128)(2,1)S(1)}, u32[]{:S(2)}, u32[]{:S(2)}) collective-permute-start(bf16[4,40,256]{2,1,0:T(8,128)(2,1)S(1)} %pad_maximum_fusion.3), channel_id=1, source_target_pairs={{0,8},{4,12},{8,0},{12,4},{1,9},{5,13},{9,1},{13,5},{2,10},{6,14},... | collective-permute-start | bytes 245768 | tf_op jit(solution)/shard_map/ppermute | solution.py:613
  15.4 1.5 %collective-permute-start.4 = (bf16[8,40,256]{2,1,0:T(8,128)(2,1)S(1)}, bf16[8,40,256]{2,1,0:T(8,128)(2,1)S(1)}, u32[]{:S(2)}, u32[]{:S(2)}) collective-permute-start(bf16[8,40,256]{2,1,0:T(8,128)(2,1)S(1)} %pad_maximum_fusion.2), channel_id=1, source_target_pairs={{0,4},{4,0},{8,12},{12,8},{1,5},{5,1},{9,13},{13,9},{2,6},{6,2},{1... | collective-permute-start | bytes 491528 | tf_op jit(solution)/shard_map/ppermute | solution.py:613
